TPU v7x, 16 devices: a whole 2x2x2 slice. The times are simulated.
16 devices in a mesh: tp: 2 (over z), dp: 8 (over y, x, core).
Axes of the slice: x: 2, y: 2, z: 2, core: 2. Of those that a mesh axis runs over, the one named last changes fastest.
Arguments:
- hidden: bfloat16 [8192, 960], P('dp')
- norm_w: bfloat16 [960], replicated
- emb_table: bfloat16 [49152, 960], P('tp')
- teacher: bfloat16 [8192, 49152], P('dp', 'tp')
- loss_mask: int32 [8192], P('dp')
Outputs:
- output 1: float32 [], replicated
- output 2: bfloat16 [8192, 960], P('dp')
- output 3: float32 [49152, 960], P('tp', 'dp')
- output 4: float32 [960], replicated
All inputs are finite; a program needn't handle non-finite values.
Results may differ from a plain program's by a relative error of at most 0.00103912.
Values sent between devices are 32-bit elements.
A program may use at most 1 GiB of HBM per device.

v0:
```python
import jax
import jax.numpy as jnp
from jax import lax
from jax.sharding import PartitionSpec as P

SOFT_CAP = 30.0
NORM_EPS = 1e-6


def rms_norm(hid_f32, scale_f32):
    inv_rms = lax.rsqrt(jnp.mean(hid_f32 * hid_f32, axis=-1, keepdims=True) + NORM_EPS)
    return hid_f32 * inv_rms * (1.0 + scale_f32)


def solution(mesh):
    def device_fn(hid_loc, norm_w, emb_loc, teach_loc, mask_loc):
        mask_f32 = mask_loc.astype(jnp.float32)
        tok_count = lax.psum(jnp.sum(mask_f32), 'dp')
        weight = mask_f32 / tok_count
        normed_f32, norm_pull = jax.vjp(rms_norm, hid_loc.astype(jnp.float32), norm_w.astype(jnp.float32))
        normed = normed_f32.astype(jnp.bfloat16)
        raw_logit = jnp.einsum('nd,vd->nv', normed, emb_loc, preferred_element_type=jnp.float32)
        tanh_val = jnp.tanh(raw_logit / SOFT_CAP)
        capped = SOFT_CAP * tanh_val
        teach_f32 = teach_loc.astype(jnp.float32)
        maxima = lax.pmax(jnp.stack([jnp.max(capped, axis=-1), jnp.max(teach_f32, axis=-1)], axis=-1), 'tp')
        stu_exp = jnp.exp(capped - maxima[:, 0:1])
        tea_exp = jnp.exp(teach_f32 - maxima[:, 1:2])
        local_sums = jnp.stack([jnp.sum(stu_exp, axis=-1), jnp.sum(tea_exp, axis=-1), jnp.sum(tea_exp * (teach_f32 - capped), axis=-1)], axis=-1)
        totals = lax.psum(local_sums, 'tp')
        lse_stu = maxima[:, 0] + jnp.log(totals[:, 0])
        lse_tea = maxima[:, 1] + jnp.log(totals[:, 1])
        kl_tok = totals[:, 2] / totals[:, 1] - lse_tea + lse_stu
        loss_val = lax.psum(jnp.sum(weight * kl_tok), 'dp')
        prob_diff = stu_exp / totals[:, 0:1] - tea_exp / totals[:, 1:2]
        d_raw = (prob_diff * weight[:, None] * (1.0 - tanh_val * tanh_val)).astype(jnp.bfloat16)
        grad_normed = lax.psum(jnp.dot(d_raw, emb_loc, preferred_element_type=jnp.float32), 'tp')
        emb_part = jnp.einsum('nv,nd->vd', d_raw, normed, preferred_element_type=jnp.float32)
        grad_emb = lax.psum_scatter(emb_part, 'dp', scatter_dimension=1, tiled=True)
        grad_hid, grad_scale = norm_pull(grad_normed)
        grad_w = lax.psum(grad_scale, 'dp')
        return loss_val, grad_hid.astype(jnp.bfloat16), grad_emb, grad_w

    return jax.shard_map(device_fn, mesh=mesh, in_specs=(P('dp', None), P(None), P('tp', None), P('dp', 'tp'), P('dp')), out_specs=(P(), P('dp', None), P('tp', 'dp'), P(None)), check_vma=False)
```

profile of v0, /device:TPU:0, one launch (start us, length us, event | category | flops | bytes accessed | tf_op | source)
XLA Modules:
  0.0 905.9 jit_solution(11702104517128002111)
XLA Ops:
  8.0 0.0 all-reduce.3.cloned.1.call-start
  8.1 1.4 convert_reduce_fusion
  9.5 16.0 %psum.35 = f32[]{:T(128)} all-reduce(f32[]{:T(128)} %convert_reduce_fusion), channel_id=1, replica_groups=mesh['tp'=2,'dp'=8] {'dp'}, use_global_device_ids=true, to_apply=%region_1.0 | all-reduce | flops 1 | bytes 8 | tf_op jit(solution)/shard_map/psum | solution.py:18
  25.5 16.0 %reduce_max.26 = bf16[1024]{0:T(1024)(128)(2,1)S(1)} reduce(bf16[1024,24576]{1,0:T(8,128)(2,1)} %param.8, bf16[]{:T(256)} %constant.19.clone.1), dimensions={1}, to_apply=%region_4.0 | reduce | flops 25164800 | bytes 50333696 | tf_op jit(solution)/shard_map/reduce_max | solution.py:26
  41.6 0.4 fusion.17
  42.0 0.6 copy-done.6
  42.6 0.6 copy-done.4
  43.2 1.8 fusion.22.clone.4
  45.0 70.2 %fusion.11 = (f32[1024]{0:T(1024)S(1)}, f32[1024,24576]{1,0:T(8,128)}) fusion(bf16[24576,960]{0,1:T(8,128)(2,1)} %param.7, bf16[1024,960]{0,1:T(8,128)(2,1)} %fusion.22.clone.4), kind=kOutput, calls=%fused_computation.15 | convolution fusion | flops 48393879552 | bytes 149819392 | tf_op jit(solution)/shard_map/nd,vd->nv/dot_general | solution.py:22
  115.2 5.0 pmax.7
  120.2 79.2 %fusion.10 = (f32[1024]{0:T(1024)S(1)}, f32[1024]{0:T(1024)S(1)}, f32[1024]{0:T(1024)S(1)}) fusion(f32[1024,24576]{1,0:T(8,128)} %get-tuple-element.19, f32[1024]{0:T(1024)S(1)} %bitcast.20, f32[1024]{0:T(1024)S(1)} %bitcast.17, bf16[1024,24576]{1,0:T(8,128)(2,1)} %param.8), kind=kLoop, calls=%fused_computation.14 | loop fusion | flops 251655168 | bytes 151015424 | tf_op jit(solution)/shard_map/reduce_sum | solution.py:29
  199.5 8.3 psum.36
  207.8 1.3 multiply_reduce_fusion
  209.0 69.3 %fusion.8 = bf16[1024,24576]{1,0:T(8,128)(2,1)} fusion(bf16[1024,24576]{1,0:T(8,128)(2,1)} %param.8, f32[1024,24576]{1,0:T(8,128)} %get-tuple-element.19, f32[1024]{0:T(1024)S(1)} %get-tuple-element.12, f32[1024]{0:T(1024)S(1)} %bitcast.26, f32[1024]{0:T(1024)S(1)} %bitcast.24, f32[1024]{0:T(1024)S(1)} %bitcast.19, f32[1024]{0:T(1024)S(1)} %bitcast.22), kind=kLoop, calls=%fused_computation.12 | loop fusion | flops 327155712 | bytes 201347072 | tf_op jit(solution)/shard_map/convert_element_type | solution.py:36
  278.3 57.0 %fusion.26 = f32[1024,960]{0,1:T(8,128)} fusion(bf16[1024,24576]{1,0:T(8,128)(2,1)} %fusion.8, bf16[24576,960]{0,1:T(8,128)(2,1)} %param.7), kind=kOutput, calls=%fused_computation.41 | convolution fusion | flops 48318382080 | bytes 101449728 | tf_op jit(solution)/shard_map/dot_general | solution.py:37
  335.3 0.0 all-reduce.3.cloned.1.call-update
  335.4 0.3 reduce-scatter.2.cloned.1.call-start
  335.7 60.7 %fusion.19 = f32[24576,960]{0,1:T(8,128)} fusion(bf16[1024,24576]{1,0:T(8,128)(2,1)} %fusion.8, bf16[1024,960]{0,1:T(8,128)(2,1)S(1)} %copy-done.1, f32[960]{0:T(1024)S(1)} %copy-done.3, f32[1024]{0:T(1024)S(1)} %copy-done.5), kind=kOutput, calls=%fused_computation.28 | convolution fusion | flops 48322314240 | bytes 146677504 | tf_op jit(solution)/shard_map/nv,nd->vd/dot_general | solution.py:38
  396.4 0.0 reduce-scatter.2.cloned.1.call-update
  396.4 36.1 %all-reduce.3.cloned.1.call-done = f32[1024,960]{0,1:T(8,128)} async-done(((f32[1024,960]{0,1:T(8,128)}), f32[1024,960]{0,1:T(8,128)}) %all-reduce.3.cloned.1.call-update) | async-done | bytes 3932176 | tf_op jit(solution)/shard_map/psum | solution.py:37
  432.6 3.4 fusion.15
  435.9 14.3 %all-reduce = (f32[]{:T(128)}, f32[960]{0:T(1024)}) all-reduce(f32[]{:T(128)} %get-tuple-element.11, f32[960]{0:T(1024)S(1)} %get-tuple-element.7), channel_id=1, replica_groups=mesh['tp'=2,'dp'=8] {'dp'}, use_global_device_ids=true, to_apply=%region_11.0 | all-reduce | flops 961 | bytes 7688 | tf_op jit(solution)/shard_map/psum | solution.py:34
  450.2 4.3 fusion.16
  454.5 443.9 %reduce-scatter.2.cloned.1.call-done = f32[24576,120]{0,1:T(8,128)} async-done(((f32[24576,960]{0,1:T(8,128)}), f32[24576,120]{0,1:T(8,128)}) %reduce-scatter.2.cloned.1.call-update) | async-done | bytes 11796496 | tf_op jit(solution)/shard_map/reduce_scatter | solution.py:39
  (26 shorter events, 0.1 us)
Async XLA Ops:
  8.0 33.5 %copy-start.9 = (bf16[960]{0:T(1024)(128)(2,1)S(1)}, bf16[960]{0:T(1024)(128)(2,1)}, u32[]{:S(2)}) copy-start(bf16[960]{0:T(1024)(128)(2,1)} %param.6) | copy-start | bytes 5764
  8.0 33.5 %copy-start = (bf16[1024,960]{0,1:T(8,128)(2,1)S(1)}, bf16[1024,960]{0,1:T(8,128)(2,1)}, u32[]{:S(2)}) copy-start(bf16[1024,960]{0,1:T(8,128)(2,1)} %param.5) | copy-start | bytes 5898244
  8.0 424.5 %all-reduce.3.cloned.1.call-start = ((), (), s32[]{:S(2)}) async-start(), calls=%async_computation.1 | async-start | bytes 7864320 | tf_op jit(solution)/shard_map/psum | solution.py:37
  41.6 1.1 copy-start.2
  42.0 0.6 copy-start.6
  42.6 0.6 copy-start.4
  120.2 87.5 %copy-start.8 = (s32[1024]{0:T(1024)S(1)}, s32[1024]{0:T(1024)}, u32[]{:S(2)}) copy-start(s32[1024]{0:T(1024)} %param.9) | copy-start | bytes 12292
  278.3 57.3 %copy-start.1 = (bf16[1024,960]{0,1:T(8,128)(2,1)S(1)}, bf16[1024,960]{0,1:T(8,128)(2,1)}, u32[]{:S(2)}) copy-start(bf16[1024,960]{0,1:T(8,128)(2,1)} %param.5) | copy-start | bytes 5898244
  278.3 57.3 %copy-start.3 = (f32[960]{0:T(1024)S(1)}, f32[960]{0:T(1024)}, u32[]{:S(2)}) copy-start(f32[960]{0:T(1024)} %copy-done.2) | copy-start | bytes 11524
  278.3 57.3 %copy-start.5 = (f32[1024]{0:T(1024)S(1)}, f32[1024]{0:T(1024)}, u32[]{:S(2)}) copy-start(f32[1024]{0:T(1024)} %copy-done.4) | copy-start | bytes 12292
  335.4 563.1 %reduce-scatter.2.cloned.1.call-start = ((), (), s32[]{:S(2)}) async-start(), calls=%async_computation.2 | async-start | bytes 106168320 | tf_op jit(solution)/shard_map/reduce_scatter | solution.py:39
  396.4 53.8 %copy-start.7 = (f32[1024]{0:T(1024)S(1)}, f32[1024]{0:T(1024)}, u32[]{:S(2)}) copy-start(f32[1024]{0:T(1024)} %copy-done.6) | copy-start | bytes 12292
Sparse Core Ops, SparseCore 0:
  335.5 97.0 all-reduce.2
Sparse Core Ops, SparseCore 1:
  396.5 501.8 reduce-scatter.1
where the time goes:
time: 906 us
  waiting for transfers between devices  480 us (53%)
  matrix products  188 us (21%)
  other arithmetic  177 us (20%)
  blocking collectives  43.6 us (5%)
  between operations  15.6 us (2%)
    reduce_scatter x1, waiting for transfers between devices, device_fn(): grad_emb = lax.psum_scatter(emb_part, 'dp', scatter_dimension=1, tiled=True)  444 us
    reduce_sum x1, other arithmetic, device_fn(): jnp.sum(stu_exp, axis=-1)  79.2 us
    dot_general x1, matrix products, device_fn(): jnp.einsum('nd,vd->nv', normed, emb_loc, preferred_element_type=jnp.float32)  70.2 us
    convert_element_type x1, other arithmetic, device_fn(): (prob_diff * weight[:, None] * (1.0 - tanh_val * tanh_val)).astype(jnp.bf...  69.3 us
    dot_general x1, matrix products, device_fn(): jnp.einsum('nv,nd->vd', d_raw, normed, preferred_element_type=jnp.float32)  60.7 us
    dot_general x1, matrix products, device_fn(): jnp.dot(d_raw, emb_loc, preferred_element_type=jnp.float32)  57 us
    psum x1, waiting for transfers between devices, device_fn(): lax.psum(jnp.dot(d_raw, emb_loc, preferred_element_type=jnp.float32), 'tp')  36.1 us
  transfers between devices with their start and end apart: 2, of which 2 were waited for; matrix products, arithmetic and copies ran while one was open for 8% of the time, Pallas kernels for 0%

commit v1 on v0

v1 whole, which is shorter than its diff:
```python
import functools

import jax
import jax.numpy as jnp
from jax import lax
from jax.experimental import pallas as pl
from jax.experimental.pallas import tpu as pltpu
from jax.sharding import PartitionSpec as P


SOFT_CAP = 30.0
NORM_EPS = 1e-6
LOG2E = 1.4426950408889634
TILE = 512
STRIP = 256
SUB = 16
LANES = 128
CHUNK_TILES = (2, 6, 10, 12, 10, 6, 2)
LOWEST = -3.0e38
VMEM_LIMIT = 60 * 1024 * 1024


def rms_norm(hid_f32, scale_f32):
    inv_rms = lax.rsqrt(jnp.mean(hid_f32 * hid_f32, axis=-1, keepdims=True) + NORM_EPS)
    return hid_f32 * inv_rms * (1.0 + scale_f32)


def params():
    return pltpu.CompilerParams(dimension_semantics=("arbitrary",), vmem_limit_bytes=VMEM_LIMIT)


def stats_kernel(steps, g_ref, e_ref, t_ref, out_ref, m_ref, zs_ref, zt_ref, kl_ref):
    step = pl.program_id(0)

    @pl.when(step == 0)
    def _():
        m_ref[...] = jnp.full(m_ref.shape, LOWEST, jnp.float32)
        zs_ref[...] = jnp.zeros_like(zs_ref)
        zt_ref[...] = jnp.zeros_like(zt_ref)
        kl_ref[...] = jnp.zeros_like(kl_ref)

    groups = TILE // LANES
    tokens = g_ref.shape[0]

    def logits(strip):
        return jnp.dot(g_ref[pl.ds(strip * STRIP, STRIP), :], e_ref[...], preferred_element_type=jnp.float32)

    raw = logits(0)
    for strip in range(tokens // STRIP):
        following = logits(strip + 1) if (strip + 1) * STRIP < tokens else None
        for sub in range(STRIP // SUB):
            rows = pl.ds(strip * STRIP + sub * SUB, SUB)
            block = raw[sub * SUB:(sub + 1) * SUB]
            tea = t_ref[rows, :].astype(jnp.float32)
            parts = [tea[:, k * LANES:(k + 1) * LANES] for k in range(groups)]
            top = m_ref[rows, :]
            old = top
            for part in parts:
                top = jnp.maximum(top, part)
            decay = jnp.exp2((old - top) * LOG2E)
            zs = zs_ref[rows, :]
            zt = zt_ref[rows, :] * decay
            kl = kl_ref[rows, :] * decay
            for k, part in enumerate(parts):
                tanh_val = jnp.tanh(block[:, k * LANES:(k + 1) * LANES] * (1.0 / SOFT_CAP))
                zs = zs + jnp.exp2(tanh_val * (SOFT_CAP * LOG2E))
                ex = jnp.exp2((part - top) * LOG2E)
                zt = zt + ex
                kl = kl + ex * (part - SOFT_CAP * tanh_val)
            m_ref[rows, :] = top
            zs_ref[rows, :] = zs
            zt_ref[rows, :] = zt
            kl_ref[rows, :] = kl
        raw = following

    @pl.when(step == steps - 1)
    def _():
        lane_max = m_ref[...]
        top = jnp.max(lane_max, axis=-1, keepdims=True)
        decay = jnp.exp2((lane_max - top) * LOG2E)
        zs = jnp.sum(zs_ref[...], axis=-1, keepdims=True)
        zt = jnp.sum(zt_ref[...] * decay, axis=-1, keepdims=True)
        kl = jnp.sum(kl_ref[...] * decay, axis=-1, keepdims=True)
        lane = lax.broadcasted_iota(jnp.int32, lane_max.shape, 1)
        packed = jnp.where(lane == 0, top, jnp.where(lane == 1, zs, jnp.where(lane == 2, zt, kl)))
        out_ref[...] = packed.T[:8, :]


def run_stats(normed, emb_t, teach):
    tokens, dim = normed.shape
    vocab = emb_t.shape[1]
    steps = vocab // TILE
    return pl.pallas_call(
        functools.partial(stats_kernel, steps),
        name="stats",
        grid=(steps,),
        out_shape=jax.ShapeDtypeStruct((8, tokens), jnp.float32),
        in_specs=[
            pl.BlockSpec((tokens, dim), lambda j: (0, 0)),
            pl.BlockSpec((dim, TILE), lambda j: (0, j)),
            pl.BlockSpec((tokens, TILE), lambda j: (0, j)),
        ],
        out_specs=pl.BlockSpec((8, tokens), lambda j: (0, 0)),
        scratch_shapes=[pltpu.VMEM((tokens, LANES), jnp.float32)] * 4,
        compiler_params=params(),
        cost_estimate=pl.CostEstimate(flops=2 * tokens * dim * vocab, bytes_accessed=2 * vocab * (tokens + dim), transcendentals=3 * tokens * vocab),
    )(normed, emb_t, teach)


def a_kernel(order_ref, prev_ref, coef_ref, g_ref, gp_ref, e_ref, t_ref, dr_ref, pp_ref, dg_ref, tok_ref):
    @pl.when(pl.program_id(0) == 0)
    def _():
        dg_ref[...] = prev_ref[...]
        tok_ref[...] = jnp.zeros_like(tok_ref)

    groups = TILE // LANES
    tokens = g_ref.shape[0]

    def logits(strip):
        return jnp.dot(g_ref[pl.ds(strip * STRIP, STRIP), :], e_ref[...], preferred_element_type=jnp.float32)

    raw = logits(0)
    for strip in range(tokens // STRIP):
        following = logits(strip + 1) if (strip + 1) * STRIP < tokens else None
        for sub in range(STRIP // SUB):
            rows = pl.ds(strip * STRIP + sub * SUB, SUB)
            block = raw[sub * SUB:(sub + 1) * SUB]
            tea = t_ref[rows, :].astype(jnp.float32)
            top = coef_ref[0, rows, :]
            stu_w = coef_ref[1, rows, :]
            tea_w = coef_ref[2, rows, :]
            for k in range(groups):
                cols = slice(k * LANES, (k + 1) * LANES)
                tanh_val = jnp.tanh(block[:, cols] * (1.0 / SOFT_CAP))
                stu = jnp.exp2(tanh_val * (SOFT_CAP * LOG2E)) * stu_w
                soft = jnp.exp2((tea[:, cols] - top) * LOG2E) * tea_w
                d_raw = (stu - soft) * (1.0 - tanh_val * tanh_val)
                dr_ref[rows, cols] = d_raw.astype(jnp.bfloat16)
        raw = following

    d_raw = dr_ref[...]
    pp_ref[...] = jnp.dot(gp_ref[0], d_raw, preferred_element_type=jnp.float32)
    dg_ref[...] += lax.dot_general(d_raw, e_ref[...], (((1,), (1,)), ((), ())), preferred_element_type=jnp.float32)


def run_a(first, tiles, order, prev, coef, normed, g_partner, emb_t, teach):
    tokens, dim = normed.shape
    half = tiles // 2
    width = tiles * TILE
    rows = g_partner.shape[1]
    return pl.pallas_call(
        a_kernel,
        name="dlogits",
        grid=(tiles,),
        out_shape=[
            jax.ShapeDtypeStruct((tokens, width), jnp.bfloat16),
            jax.ShapeDtypeStruct((rows, width), jnp.float32),
            jax.ShapeDtypeStruct((tokens, dim), jnp.float32),
            jax.ShapeDtypeStruct((8, LANES), jnp.float32),
        ],
        in_specs=[
            pl.BlockSpec((8, LANES), lambda j: (0, 0)),
            pl.BlockSpec((tokens, dim), lambda j: (0, 0)),
            pl.BlockSpec((3, tokens, LANES), lambda j: (0, 0, 0)),
            pl.BlockSpec((tokens, dim), lambda j: (0, 0)),
            pl.BlockSpec((1, rows, tokens), lambda j: (j // half, 0, 0)),
            pl.BlockSpec((dim, TILE), lambda j: (0, first + j)),
            pl.BlockSpec((tokens, TILE), lambda j: (0, first + j)),
        ],
        out_specs=[
            pl.BlockSpec((tokens, TILE), lambda j: (0, j)),
            pl.BlockSpec((rows, TILE), lambda j: (0, j)),
            pl.BlockSpec((tokens, dim), lambda j: (0, 0)),
            pl.BlockSpec((8, LANES), lambda j: (0, 0)),
        ],
        compiler_params=params(),
        cost_estimate=pl.CostEstimate(flops=5 * tokens * dim * width, bytes_accessed=10 * tokens * width, transcendentals=3 * tokens * width),
    )(order, prev, coef, normed, g_partner, emb_t, teach)


def b_kernel(half, order_ref, go_ref, dr_ref, r_ref, keep_ref, send0_ref, send1_ref, tok_ref):
    step = pl.program_id(0)
    total = jnp.dot(go_ref[0], dr_ref[...], preferred_element_type=jnp.float32) + r_ref[...]
    mid = keep_ref.shape[0]
    keep_ref[...] = total[:mid]

    @pl.when(step == 0)
    def _():
        tok_ref[...] = jnp.zeros_like(tok_ref)

    @pl.when(step < half)
    def _():
        send0_ref[...] = total[mid:]

    @pl.when(step >= half)
    def _():
        send1_ref[...] = total[mid:]


def run_b(tiles, order, g_own, d_raw, recv):
    tokens = d_raw.shape[0]
    rows = g_own.shape[1]
    half = tiles // 2
    width = tiles * TILE
    lower = lambda j: (0, jnp.minimum(j, half - 1))
    upper = lambda j: (0, jnp.maximum(j - half, 0))
    return pl.pallas_call(
        functools.partial(b_kernel, half),
        name="own_half",
        grid=(tiles,),
        out_shape=[
            jax.ShapeDtypeStruct((rows // 2, width), jnp.float32),
            jax.ShapeDtypeStruct((rows // 2, width // 2), jnp.float32),
            jax.ShapeDtypeStruct((rows // 2, width // 2), jnp.float32),
            jax.ShapeDtypeStruct((8, LANES), jnp.float32),
        ],
        in_specs=[
            pl.BlockSpec((8, LANES), lambda j: (0, 0)),
            pl.BlockSpec((1, rows, tokens), lambda j: (j // half, 0, 0)),
            pl.BlockSpec((tokens, TILE), lambda j: (0, j)),
            pl.BlockSpec((rows, TILE), lambda j: (0, j)),
        ],
        out_specs=[
            pl.BlockSpec((rows // 2, TILE), lambda j: (0, j)),
            pl.BlockSpec((rows // 2, TILE), lower),
            pl.BlockSpec((rows // 2, TILE), upper),
            pl.BlockSpec((8, LANES), lambda j: (0, 0)),
        ],
        compiler_params=params(),
        cost_estimate=pl.CostEstimate(flops=2 * tokens * rows * width, bytes_accessed=width * (2 * tokens + 8 * rows), transcendentals=0),
    )(order, g_own, d_raw, recv)


def relay_kernel(half, order_ref, keep_ref, rx_ref, ry_ref, last0_ref, last1_ref, tok_ref):
    step = pl.program_id(0)

    @pl.when(step == 0)
    def _():
        tok_ref[...] = jnp.zeros_like(tok_ref)

    @pl.when(step < half)
    def _():
        last0_ref[...] = keep_ref[...] + rx_ref[...]

    @pl.when(step >= half)
    def _():
        last1_ref[...] = keep_ref[...] + ry_ref[...]


def run_relay(tiles, order, keep, rx, ry):
    rows = keep.shape[0] // 2
    half = tiles // 2
    width = half * TILE
    lower = lambda j: jnp.minimum(j, half - 1)
    upper = lambda j: jnp.maximum(j - half, 0)
    return pl.pallas_call(
        functools.partial(relay_kernel, half),
        name="relay",
        grid=(tiles,),
        out_shape=[
            jax.ShapeDtypeStruct((rows, width), jnp.float32),
            jax.ShapeDtypeStruct((rows, width), jnp.float32),
            jax.ShapeDtypeStruct((8, LANES), jnp.float32),
        ],
        in_specs=[
            pl.BlockSpec((8, LANES), lambda j: (0, 0)),
            pl.BlockSpec((rows, TILE), lambda j: (1, j)),
            pl.BlockSpec((rows, TILE), lambda j: (1, lower(j))),
            pl.BlockSpec((rows, TILE), lambda j: (1, upper(j))),
        ],
        out_specs=[
            pl.BlockSpec((rows, TILE), lambda j: (0, lower(j))),
            pl.BlockSpec((rows, TILE), lambda j: (0, upper(j))),
            pl.BlockSpec((8, LANES), lambda j: (0, 0)),
        ],
        compiler_params=params(),
        cost_estimate=pl.CostEstimate(flops=600 * rows * tiles * TILE, bytes_accessed=12 * rows * tiles * TILE, transcendentals=0),
    )(order, keep, rx, ry)


def final_kernel(half, buf_ref, order_ref, keep_ref, rx_ref, ry_ref, last0_ref, last1_ref, out_ref):
    step = pl.program_id(0)

    @pl.when(step < half)
    def _():
        out_ref[...] = keep_ref[...] + rx_ref[...] + last0_ref[...]

    @pl.when(step >= half)
    def _():
        out_ref[...] = keep_ref[...] + ry_ref[...] + last1_ref[...]


def run_final(first, tiles, vocab, order, buf, keep, rx, ry, last0, last1):
    rows = last0.shape[0]
    half = tiles // 2
    lower = lambda j: (0, jnp.minimum(j, half - 1))
    upper = lambda j: (0, jnp.maximum(j - half, 0))
    specs = [
        pl.BlockSpec((8, LANES), lambda j: (0, 0)),
        pl.BlockSpec((rows, TILE), lambda j: (0, j)),
        pl.BlockSpec((rows, TILE), lower),
        pl.BlockSpec((rows, TILE), upper),
        pl.BlockSpec((rows, TILE), lower),
        pl.BlockSpec((rows, TILE), upper),
    ]
    body = functools.partial(final_kernel, half)
    operands = (order, keep, rx, ry, last0, last1)
    aliases = {}
    if buf is None:
        body = functools.partial(final_kernel, half, None)
    else:
        specs = [pl.BlockSpec(memory_space=pl.ANY)] + specs
        operands = (buf,) + operands
        aliases = {0: 0}
    return pl.pallas_call(
        body,
        name="finish",
        grid=(tiles,),
        out_shape=jax.ShapeDtypeStruct((rows, vocab), jnp.float32),
        in_specs=specs,
        out_specs=pl.BlockSpec((rows, TILE), lambda j: (0, first + j)),
        input_output_aliases=aliases,
        compiler_params=params(),
        cost_estimate=pl.CostEstimate(flops=600 * rows * tiles * TILE, bytes_accessed=16 * rows * tiles * TILE, transcendentals=0),
    )(*operands)


def solution(mesh):
    dp = mesh.shape['dp']
    swap = {bit: [(i, i ^ bit) for i in range(dp)] for bit in range(1, dp)}
    across = [(0, 1), (1, 0)]

    def device_fn(hid_loc, norm_w, emb_loc, teach_loc, mask_loc):
        me = lax.axis_index('dp')
        tokens, dim = hid_loc.shape
        vocab = emb_loc.shape[0]
        mask_f32 = mask_loc.astype(jnp.float32)
        count = jnp.full((8, LANES), jnp.sum(mask_f32), jnp.float32)
        tok_count = count
        for bit in range(1, dp):
            tok_count = tok_count + lax.ppermute(count, 'dp', swap[bit])
        weight = mask_f32 / tok_count[0, 0]

        normed_f32, norm_pull = jax.vjp(rms_norm, hid_loc.astype(jnp.float32), norm_w.astype(jnp.float32))
        normed = normed_f32.astype(jnp.bfloat16)
        emb_t = emb_loc.T
        mine = run_stats(normed, emb_t, teach_loc)

        blocks = normed.T.reshape(dp, dim // dp, tokens)

        def arranged(flips):
            return jnp.concatenate([lax.dynamic_index_in_dim(blocks, me ^ flip, 0, keepdims=False) for flip in flips], axis=0)

        g_own = jnp.stack([arranged((0, 4, 2, 6)), arranged((0, 2, 4, 6))])
        g_partner = jnp.stack([arranged((1, 5, 3, 7)), arranged((1, 3, 5, 7))])

        other = lax.ppermute(mine, 'tp', across)
        top = jnp.maximum(mine[0], other[0])
        mine_scale = jnp.exp(mine[0] - top)
        other_scale = jnp.exp(other[0] - top)
        sum_stu = mine[1] + other[1]
        sum_tea = mine[2] * mine_scale + other[2] * other_scale
        dot_kl = mine[3] * mine_scale + other[3] * other_scale
        kl_tok = dot_kl / sum_tea - (top + jnp.log(sum_tea)) + jnp.log(sum_stu)
        coef = jnp.stack([top, weight / sum_stu, weight / sum_tea])
        coef = jnp.broadcast_to(coef[:, :, None], (3, tokens, LANES))

        zero_token = jnp.zeros((8, LANES), jnp.float32)
        grad_part = jnp.zeros((tokens, dim), jnp.float32)
        count_chunks = len(CHUNK_TILES)
        firsts = [sum(CHUNK_TILES[:k]) for k in range(count_chunks)]
        a_token, b_token = {}, {}
        d_raw, recv, state = {}, {}, {}

        def do_a(k, grad):
            order = b_token[k - 2] if k >= 2 else zero_token
            d_raw[k], part, grad, a_token[k] = run_a(firsts[k], CHUNK_TILES[k], order, grad, coef, normed, g_partner, emb_t, teach_loc)
            recv[k] = lax.ppermute(part, 'dp', swap[1])
            return grad

        def do_b(k):
            order = a_token[min(k + 1, count_chunks - 1)]
            keep, send0, send1, b_token[k] = run_b(CHUNK_TILES[k], order, g_own, d_raw[k], recv[k])
            rx = lax.ppermute(send0, 'dp', swap[2])
            ry = lax.ppermute(send1, 'dp', swap[4])
            state[k] = (keep, rx, ry)

        grad_part = do_a(0, grad_part)
        for k in range(1, count_chunks):
            grad_part = do_a(k, grad_part)
            do_b(k - 1)
        do_b(count_chunks - 1)

        order = b_token[count_chunks - 1]
        for k in range(count_chunks):
            last0, last1, order = run_relay(CHUNK_TILES[k], order, *state[k])
            last0 = lax.ppermute(last0, 'dp', swap[4])
            last1 = lax.ppermute(last1, 'dp', swap[2])
            state[k] += (last0, last1)

        grad_other = lax.ppermute(grad_part, 'tp', across)
        grad_normed = grad_part + grad_other
        grad_hid, grad_scale = norm_pull(grad_normed)
        loss_val, grad_w = lax.psum((jnp.sum(weight * kl_tok), grad_scale), 'dp')

        grad_emb = None
        for k in range(count_chunks):
            order = order if k < count_chunks - 3 else jnp.broadcast_to(grad_w[:LANES], (8, LANES))
            grad_emb = run_final(firsts[k], CHUNK_TILES[k], vocab, order, grad_emb, *state[k])
        return loss_val, grad_hid.astype(jnp.bfloat16), grad_emb.T, grad_w

    return jax.shard_map(device_fn, mesh=mesh, in_specs=(P('dp', None), P(None), P('tp', None), P('dp', 'tp'), P('dp')), out_specs=(P(), P('dp', None), P('tp', 'dp'), P(None)), check_vma=False)
```

time: 906 us -> 850 us (0.938); the launches traced: 906 us -> 840 us
  Pallas kernels: 0 us -> 488 us
  waiting for transfers between devices: 480 us -> 236 us
  matrix products: 188 us -> 0 us
  other arithmetic: 177 us -> 19.6 us
  starting transfers between devices: 0.3 us -> 45.9 us
  local copies, waits for them, and re-layouts: 1.25 us -> 32.9 us
  blocking collectives: 43.6 us -> 16.1 us
  between operations: 15.6 us -> 1.28 us
    pallas_call x0 -> x29, Pallas kernels: none -> 488 us  [the longest x7 225 us: run_a(): pl.pallas_call(a_kernel, name='dlogits', grid=(tiles,), out_shape=[jax.Sh...]
    reduce_scatter x1 -> x0, waiting for transfers between devices: 444 us -> none  [device_fn(): grad_emb = lax.psum_scatter(emb_part, 'dp', scatter_dimension=1, tiled=True)]
    ppermute x0 -> x44, waiting for transfers between devices: none -> 236 us  [the longest x7 89.5 us: do_b(): rx = lax.ppermute(send0, 'dp', swap[2])]
    dot_general x3 -> x0, matrix products: 188 us -> none  [the longest x1 70.2 us: device_fn(): jnp.einsum('nd,vd->nv', normed, emb_loc, preferred_element_type=jnp.float32)]
    reduce_sum x3 -> x1, other arithmetic: 81.9 us -> 1.29 us  [device_fn(): count = jnp.full((8, LANES), jnp.sum(mask_f32), jnp.float32)]
    convert_element_type x2, other arithmetic: 73.6 us -> 4.17 us  [the longest x1 2.27 us: device_fn(): return (loss_val, grad_hid.astype(jnp.bfloat16), grad_emb.T, grad_w)]
    ppermute x0 -> x44, starting transfers between devices: none -> 45.9 us  [the longest x7 9.24 us: do_b(): ry = lax.ppermute(send1, 'dp', swap[4])]
    psum x1 -> x0, waiting for transfers between devices: 36.1 us -> none  [device_fn(): lax.psum(jnp.dot(d_raw, emb_loc, preferred_element_type=jnp.float32), 'tp')]
  transfers between devices with their start and end apart: 2 -> 44, of which waited for: 2 -> 11; matrix products, arithmetic and copies ran while one was open for 8% -> 5% of each run, Pallas kernels for 0% -> 56%
where the time goes in v1:
time: 850 us; the launch traced here: 840 us
  Pallas kernels  488 us (57%)
  waiting for transfers between devices  236 us (28%)
  starting transfers between devices  45.9 us (5%)
  local copies, waits for them, and re-layouts  32.9 us (4%)
  other arithmetic  19.6 us (2%)
  blocking collectives  16.1 us (2%)
    pallas_call x7, Pallas kernels, run_a(): pl.pallas_call(a_kernel, name='dlogits', grid=(tiles,), out_shape=[jax.Sh...  225 us
    pallas_call x1, Pallas kernels, run_stats(): pl.pallas_call(functools.partial(stats_kernel, steps), name='stats', grid...  101 us
    ppermute x7, waiting for transfers between devices, do_b(): rx = lax.ppermute(send0, 'dp', swap[2])  89.5 us
    pallas_call x7, Pallas kernels, run_b(): pl.pallas_call(functools.partial(b_kernel, half), name='own_half', grid=(...  83.1 us
    ppermute x7, waiting for transfers between devices, device_fn(): last0 = lax.ppermute(last0, 'dp', swap[4])  78.7 us
    ppermute x7, waiting for transfers between devices, do_b(): ry = lax.ppermute(send1, 'dp', swap[4])  48.6 us
    pallas_call x7, Pallas kernels, run_final(): pl.pallas_call(body, name='finish', grid=(tiles,), out_shape=jax.ShapeDty...  40.7 us
    pallas_call x7, Pallas kernels, run_relay(): pl.pallas_call(functools.partial(relay_kernel, half), name='relay', grid=...  38.8 us
  transfers between devices with their start and end apart: 44, of which 11 were waited for; matrix products, arithmetic and copies ran while one was open for 5% of the time, Pallas kernels for 56%

profile of v1, /device:TPU:0, one launch (start us, length us, event | category | flops | bytes accessed | tf_op | source)
XLA Modules:
  0.0 839.8 jit_solution(2564062505956497732)
XLA Ops:
  21.9 100.5 %stats.1 = f32[8,1024]{1,0:T(8,128)} custom-call(bf16[1024,960]{1,0:T(8,128)(2,1)} %fusion.2.g_ref, bf16[960,24576]{1,0:T(8,128)(2,1)} %bitcast.40, bf16[1024,24576]{1,0:T(8,128)(2,1)} %t_ref.15), custom_call_target="tpu_custom_call" | custom-call | flops 48318382080 | bytes 97517568 | tf_op jit(solution)/shard_map/stats/pallas_call | solution.py:93
  135.5 14.0 %dlogits.7 = (bf16[1024,1024]{1,0:T(8,128)(2,1)}, f32[480,1024]{1,0:T(8,128)}, f32[1024,960]{1,0:T(8,128)}, f32[8,128]{1,0:T(8,128)}) custom-call(f32[8,128]{1,0:T(8,128)} %broadcast_in_dim.26.order_ref, f32[1024,960]{1,0:T(8,128)} %broadcast_in_dim.27.prev_ref, f32[3,1024,128]{2,1,0:T(8,128)} %broadcast_in_dim.28.coef_ref, bf16[1024,960]{1,0:T(8,128)(2,1)} %fusion.2.g_ref, ...), custom_call_target="tpu_custom_call" | custom-call | flops 5033164800 | bytes 10485760 | tf_op jit(solution)/shard_map/dlogits/pallas_call | solution.py:151
  149.6 29.4 %dlogits.8 = (bf16[1024,3072]{1,0:T(8,128)(2,1)}, f32[480,3072]{1,0:T(8,128)}, f32[1024,960]{1,0:T(8,128)}, f32[8,128]{1,0:T(8,128)}) custom-call(f32[8,128]{1,0:T(8,128)} %broadcast_in_dim.26.order_ref, f32[1024,960]{1,0:T(8,128)} %get-tuple-element.79.prev_ref, f32[3,1024,128]{2,1,0:T(8,128)} %broadcast_in_dim.28.coef_ref, bf16[1024,960]{1,0:T(8,128)(2,1)} %fusion.2.g_ref, ...), custom_call_target="tpu_custom_call" | custom-call | flops 15099494400 | bytes 31457280 | tf_op jit(solution)/shard_map/dlogits/pallas_call | solution.py:151
  187.1 43.6 %dlogits.9 = (bf16[1024,5120]{1,0:T(8,128)(2,1)}, f32[480,5120]{1,0:T(8,128)}, f32[1024,960]{1,0:T(8,128)}, f32[8,128]{1,0:T(8,128)}) custom-call(f32[8,128]{1,0:T(8,128)} %get-tuple-element.83.order_ref, f32[1024,960]{1,0:T(8,128)} %get-tuple-element.84.prev_ref, f32[3,1024,128]{2,1,0:T(8,128)} %broadcast_in_dim.28.coef_ref, ...), custom_call_target="tpu_custom_call" | custom-call | flops 25165824000 | bytes 52428800 | tf_op jit(solution)/shard_map/dlogits/pallas_call | solution.py:151
  230.7 10.7 %own_half.8 = (f32[240,3072]{1,0:T(8,128)}, f32[240,1536]{1,0:T(8,128)}, f32[240,1536]{1,0:T(8,128)}, f32[8,128]{1,0:T(8,128)}) custom-call(f32[8,128]{1,0:T(8,128)} %get-tuple-element.85.order_ref, bf16[2,480,1024]{2,1,0:T(8,128)(2,1)} %pad_maximum_fusion.1.go_ref, bf16[1024,3072]{1,0:T(8,128)(2,1)} %get-tuple-element.86.dr_ref, ...), custom_call_target="tpu_custom_call" | custom-call | flops 3019898880 | bytes 18087936 | tf_op jit(solution)/shard_map/own_half/pallas_call | solution.py:207
  241.4 51.0 %dlogits.10 = (bf16[1024,6144]{1,0:T(8,128)(2,1)}, f32[480,6144]{1,0:T(8,128)}, f32[1024,960]{1,0:T(8,128)}, f32[8,128]{1,0:T(8,128)}) custom-call(f32[8,128]{1,0:T(8,128)} %get-tuple-element.88.order_ref, f32[1024,960]{1,0:T(8,128)} %get-tuple-element.89.prev_ref, f32[3,1024,128]{2,1,0:T(8,128)} %broadcast_in_dim.28.coef_ref, ...), custom_call_target="tpu_custom_call" | custom-call | flops 30198988800 | bytes 62914560 | tf_op jit(solution)/shard_map/dlogits/pallas_call | solution.py:151
  292.9 16.3 %own_half.9 = (f32[240,5120]{1,0:T(8,128)}, f32[240,2560]{1,0:T(8,128)}, f32[240,2560]{1,0:T(8,128)}, f32[8,128]{1,0:T(8,128)}) custom-call(f32[8,128]{1,0:T(8,128)} %get-tuple-element.90.order_ref, bf16[2,480,1024]{2,1,0:T(8,128)(2,1)} %pad_maximum_fusion.1.go_ref, bf16[1024,5120]{1,0:T(8,128)(2,1)} %get-tuple-element.91.dr_ref, ...), custom_call_target="tpu_custom_call" | custom-call | flops 5033164800 | bytes 30146560 | tf_op jit(solution)/shard_map/own_half/pallas_call | solution.py:207
  309.2 43.8 %dlogits.11 = (bf16[1024,5120]{1,0:T(8,128)(2,1)}, f32[480,5120]{1,0:T(8,128)}, f32[1024,960]{1,0:T(8,128)}, f32[8,128]{1,0:T(8,128)}) custom-call(f32[8,128]{1,0:T(8,128)} %get-tuple-element.93.order_ref, f32[1024,960]{1,0:T(8,128)} %get-tuple-element.94.prev_ref, f32[3,1024,128]{2,1,0:T(8,128)} %broadcast_in_dim.28.coef_ref, ...), custom_call_target="tpu_custom_call" | custom-call | flops 25165824000 | bytes 52428800 | tf_op jit(solution)/shard_map/dlogits/pallas_call | solution.py:151
  353.1 19.6 %own_half.10 = (f32[240,6144]{1,0:T(8,128)}, f32[240,3072]{1,0:T(8,128)}, f32[240,3072]{1,0:T(8,128)}, f32[8,128]{1,0:T(8,128)}) custom-call(f32[8,128]{1,0:T(8,128)} %get-tuple-element.95.order_ref, bf16[2,480,1024]{2,1,0:T(8,128)(2,1)} %pad_maximum_fusion.1.go_ref, bf16[1024,6144]{1,0:T(8,128)(2,1)} %get-tuple-element.96.dr_ref, ...), custom_call_target="tpu_custom_call" | custom-call | flops 6039797760 | bytes 36175872 | tf_op jit(solution)/shard_map/own_half/pallas_call | solution.py:207
  372.7 29.0 %dlogits.12 = (bf16[1024,3072]{1,0:T(8,128)(2,1)}, f32[480,3072]{1,0:T(8,128)}, f32[1024,960]{1,0:T(8,128)}, f32[8,128]{1,0:T(8,128)}) custom-call(f32[8,128]{1,0:T(8,128)} %get-tuple-element.98.order_ref, f32[1024,960]{1,0:T(8,128)} %get-tuple-element.99.prev_ref, f32[3,1024,128]{2,1,0:T(8,128)} %broadcast_in_dim.28.coef_ref, ...), custom_call_target="tpu_custom_call" | custom-call | flops 15099494400 | bytes 31457280 | tf_op jit(solution)/shard_map/dlogits/pallas_call | solution.py:151
  406.0 10.3 %collective-permute-done.15.rx_ref = f32[240,512]{1,0:T(8,128)S(1)} collective-permute-done((f32[240,512]{1,0:T(8,128)S(1)}, f32[240,512]{1,0:T(8,128)S(1)}, u32[]{:S(2)}, u32[]{:S(2)}) %collective-permute-start.15) | collective-permute-done | bytes 491552 | tf_op jit(solution)/shard_map/ppermute | solution.py:384
  418.1 30.7 %collective-permute-done.16.ry_ref = f32[240,512]{1,0:T(8,128)S(1)} collective-permute-done((f32[240,512]{1,0:T(8,128)S(1)}, f32[240,512]{1,0:T(8,128)S(1)}, u32[]{:S(2)}, u32[]{:S(2)}) %collective-permute-start.16) | collective-permute-done | bytes 491552 | tf_op jit(solution)/shard_map/ppermute | solution.py:385
  454.0 16.4 %own_half.11 = (f32[240,5120]{1,0:T(8,128)}, f32[240,2560]{1,0:T(8,128)}, f32[240,2560]{1,0:T(8,128)}, f32[8,128]{1,0:T(8,128)}) custom-call(f32[8,128]{1,0:T(8,128)} %get-tuple-element.100.order_ref, bf16[2,480,1024]{2,1,0:T(8,128)(2,1)} %pad_maximum_fusion.1.go_ref, bf16[1024,5120]{1,0:T(8,128)(2,1)} %get-tuple-element.101.dr_ref, ...), custom_call_target="tpu_custom_call" | custom-call | flops 5033164800 | bytes 30146560 | tf_op jit(solution)/shard_map/own_half/pallas_call | solution.py:207
  470.3 14.1 %dlogits.13 = (bf16[1024,1024]{1,0:T(8,128)(2,1)}, f32[480,1024]{1,0:T(8,128)}, f32[1024,960]{1,0:T(8,128)}, f32[8,128]{1,0:T(8,128)}) custom-call(f32[8,128]{1,0:T(8,128)} %get-tuple-element.103.order_ref, f32[1024,960]{1,0:T(8,128)} %get-tuple-element.104.prev_ref, f32[3,1024,128]{2,1,0:T(8,128)} %broadcast_in_dim.28.coef_ref, ...), custom_call_target="tpu_custom_call" | custom-call | flops 5033164800 | bytes 10485760 | tf_op jit(solution)/shard_map/dlogits/pallas_call | solution.py:151
  484.4 20.9 %collective-permute-done.19.rx_ref = f32[240,2560]{1,0:T(8,128)} collective-permute-done((f32[240,2560]{1,0:T(8,128)}, f32[240,2560]{1,0:T(8,128)}, u32[]{:S(2)}, u32[]{:S(2)}) %collective-permute-start.19) | collective-permute-done | bytes 2457632 | tf_op jit(solution)/shard_map/ppermute | solution.py:384
  510.2 58.2 %collective-permute-done.21.rx_ref = f32[240,3072]{1,0:T(8,128)S(1)} collective-permute-done((f32[240,3072]{1,0:T(8,128)}, f32[240,3072]{1,0:T(8,128)S(1)}, u32[]{:S(2)}, u32[]{:S(2)}) %collective-permute-start.21) | collective-permute-done | bytes 2949152 | tf_op jit(solution)/shard_map/ppermute | solution.py:384
  586.8 39.9 %collective-permute-done.30.last0_ref = f32[120,512]{1,0:T(8,128)S(1)} collective-permute-done((f32[120,512]{1,0:T(8,128)}, f32[120,512]{1,0:T(8,128)S(1)}, u32[]{:S(2)}, u32[]{:S(2)}) %collective-permute-start.30) | collective-permute-done | bytes 245792 | tf_op jit(solution)/shard_map/ppermute | solution.py:397
  630.5 10.5 %own_half.13 = (f32[240,3072]{1,0:T(8,128)}, f32[240,1536]{1,0:T(8,128)}, f32[240,1536]{1,0:T(8,128)}, f32[8,128]{1,0:T(8,128)}) custom-call(f32[8,128]{1,0:T(8,128)} %get-tuple-element.106.order_ref, bf16[2,480,1024]{2,1,0:T(8,128)(2,1)} %pad_maximum_fusion.1.go_ref, bf16[1024,3072]{1,0:T(8,128)(2,1)} %get-tuple-element.130.dr_ref, ...), custom_call_target="tpu_custom_call" | custom-call | flops 3019898880 | bytes 18087936 | tf_op jit(solution)/shard_map/own_half/pallas_call | solution.py:207
  657.9 38.8 %collective-permute-done.32.last0_ref = f32[120,1536]{1,0:T(8,128)S(1)} collective-permute-done((f32[120,1536]{1,0:T(8,128)S(1)}, f32[120,1536]{1,0:T(8,128)S(1)}, u32[]{:S(2)}, u32[]{:S(2)}) %collective-permute-start.32) | collective-permute-done | bytes 737312 | tf_op jit(solution)/shard_map/ppermute | solution.py:397
  698.1 8.9 %relay.10 = (f32[120,3072]{1,0:T(8,128)}, f32[120,3072]{1,0:T(8,128)}, f32[8,128]{1,0:T(8,128)}) custom-call(f32[8,128]{1,0:T(8,128)} %get-tuple-element.121.order_ref, f32[240,6144]{1,0:T(8,128)} %get-tuple-element.122.keep_ref, f32[240,3072]{1,0:T(8,128)} %copy-done.4, f32[240,3072]{1,0:T(8,128)} %collective-permute-done.22.ry_ref), custom_call_target="tpu_custom_call" | custom-call | flops 442368000 | bytes 8847360 | tf_op jit(solution)/shard_map/relay/pallas_call | solution.py:256
  718.2 14.7 %collective-permute-done.27.ry_ref = f32[240,1536]{1,0:T(8,128)S(1)} collective-permute-done((f32[240,1536]{1,0:T(8,128)}, f32[240,1536]{1,0:T(8,128)S(1)}, u32[]{:S(2)}, u32[]{:S(2)}) %collective-permute-start.27) | collective-permute-done | bytes 1474592 | tf_op jit(solution)/shard_map/ppermute | solution.py:385
  748.9 18.5 %collective-permute-done.35.last1_ref = f32[120,2560]{1,0:T(8,128)} collective-permute-done((f32[120,2560]{1,0:T(8,128)}, f32[120,2560]{1,0:T(8,128)}, u32[]{:S(2)}, u32[]{:S(2)}) %collective-permute-start.35) | collective-permute-done | bytes 1228832 | tf_op jit(solution)/shard_map/ppermute | solution.py:398
  778.6 9.3 %finish.10.buf_ref = f32[120,24576]{1,0:T(8,128)} custom-call(f32[120,24576]{1,0:T(8,128)} %finish.9.buf_ref, f32[8,128]{1,0:T(8,128)} %get-tuple-element.139.order_ref, f32[240,6144]{1,0:T(8,128)} %get-tuple-element.122.keep_ref, f32[240,3072]{1,0:T(8,128)} %copy-done.4, ...), custom_call_target="tpu_custom_call", output_to_operand_aliasing={{}: (0, {})} | custom-call | flops 442368000 | bytes 11796480 | tf_op jit(solution)/shard_map/finish/pallas_call | solution.py:315
  802.8 16.1 %all-reduce = (f32[]{:T(128)}, f32[960]{0:T(1024)S(1)}) all-reduce(f32[]{:T(128)} %get-tuple-element.192, f32[960]{0:T(1024)S(1)} %get-tuple-element.166), channel_id=1, replica_groups=mesh['tp'=2,'dp'=8] {'dp'}, use_global_device_ids=true, to_apply=%region_3.4 | all-reduce | flops 961 | bytes 7688 | tf_op jit(solution)/shard_map/psum | solution.py:404
  (184 shorter events, 173.4 us)
Async XLA Ops:
  2.6 120.4 %collective-permute-start.5 = (f32[8,128]{1,0:T(8,128)S(1)}, f32[8,128]{1,0:T(8,128)S(1)}, u32[]{:S(2)}, u32[]{:S(2)}) collective-permute-start(f32[8,128]{1,0:T(8,128)S(1)} %broadcast_in_dim.12), channel_id=1, source_target_pairs={{0,6},{1,7},{2,4},{3,5},{4,2},{5,3},{6,0},{7,1},{8,14},{9,15},{10,... | collective-permute-start | bytes 12296 | tf_op jit(solution)/shard_map/ppermute | solution.py:341
  6.8 116.3 %collective-permute-start.4 = (f32[8,128]{1,0:T(8,128)S(1)}, f32[8,128]{1,0:T(8,128)S(1)}, u32[]{:S(2)}, u32[]{:S(2)}) collective-permute-start(f32[8,128]{1,0:T(8,128)S(1)} %broadcast_in_dim.12), channel_id=1, source_target_pairs={{0,5},{1,4},{2,7},{3,6},{4,1},{5,0},{6,3},{7,2},{8,13},{9,12},{10,... | collective-permute-start | bytes 12296 | tf_op jit(solution)/shard_map/ppermute | solution.py:341
  6.8 118.1 %collective-permute-start.3 = (f32[8,128]{1,0:T(8,128)S(1)}, f32[8,128]{1,0:T(8,128)S(1)}, u32[]{:S(2)}, u32[]{:S(2)}) collective-permute-start(f32[8,128]{1,0:T(8,128)S(1)} %broadcast_in_dim.12), channel_id=1, source_target_pairs={{0,4},{1,5},{2,6},{3,7},{4,0},{5,1},{6,2},{7,3},{8,12},{9,13},{10,... | collective-permute-start | bytes 12296 | tf_op jit(solution)/shard_map/ppermute | solution.py:341
  7.9 118.7 %collective-permute-start.2 = (f32[8,128]{1,0:T(8,128)S(1)}, f32[8,128]{1,0:T(8,128)S(1)}, u32[]{:S(2)}, u32[]{:S(2)}) collective-permute-start(f32[8,128]{1,0:T(8,128)S(1)} %broadcast_in_dim.12), channel_id=1, source_target_pairs={{0,3},{1,2},{2,1},{3,0},{4,7},{5,6},{6,5},{7,4},{8,11},{9,10},{10,... | collective-permute-start | bytes 12296 | tf_op jit(solution)/shard_map/ppermute | solution.py:341
  8.8 117.9 %collective-permute-start.1 = (f32[8,128]{1,0:T(8,128)S(1)}, f32[8,128]{1,0:T(8,128)S(1)}, u32[]{:S(2)}, u32[]{:S(2)}) collective-permute-start(f32[8,128]{1,0:T(8,128)S(1)} %broadcast_in_dim.12), channel_id=1, source_target_pairs={{0,2},{1,3},{2,0},{3,1},{4,6},{5,7},{6,4},{7,5},{8,10},{9,11},{10,... | collective-permute-start | bytes 12296 | tf_op jit(solution)/shard_map/ppermute | solution.py:341
  230.7 62.3 %collective-permute-start.10 = (f32[480,5120]{1,0:T(8,128)}, f32[480,5120]{1,0:T(8,128)}, u32[]{:S(2)}, u32[]{:S(2)}) collective-permute-start(f32[480,5120]{1,0:T(8,128)} %get-tuple-element.92), channel_id=1, source_target_pairs={{0,1},{1,0},{2,3},{3,2},{4,5},{5,4},{6,7},{7,6},{8,9},{9,8},{10,11... | collective-permute-start | bytes 29491208 | tf_op jit(solution)/shard_map/ppermute | solution.py:378
  292.4 60.7 %collective-permute-start.11 = (f32[480,6144]{1,0:T(8,128)}, f32[480,6144]{1,0:T(8,128)}, u32[]{:S(2)}, u32[]{:S(2)}) collective-permute-start(f32[480,6144]{1,0:T(8,128)} %get-tuple-element.97), channel_id=1, source_target_pairs={{0,1},{1,0},{2,3},{3,2},{4,5},{5,4},{6,7},{7,6},{8,9},{9,8},{10,11... | collective-permute-start | bytes 35389448 | tf_op jit(solution)/shard_map/ppermute | solution.py:378
  353.0 100.6 %collective-permute-start.12 = (f32[480,5120]{1,0:T(8,128)}, f32[480,5120]{1,0:T(8,128)}, u32[]{:S(2)}, u32[]{:S(2)}) collective-permute-start(f32[480,5120]{1,0:T(8,128)} %get-tuple-element.102), channel_id=1, source_target_pairs={{0,1},{1,0},{2,3},{3,2},{4,5},{5,4},{6,7},{7,6},{8,9},{9,8},{10,11... | collective-permute-start | bytes 29491208 | tf_op jit(solution)/shard_map/ppermute | solution.py:378
  401.8 183.5 %collective-permute-start.25 = (f32[480,3072]{1,0:T(8,128)}, f32[480,3072]{1,0:T(8,128)}, u32[]{:S(2)}, u32[]{:S(2)}) collective-permute-start(f32[480,3072]{1,0:T(8,128)} %get-tuple-element.131), channel_id=1, source_target_pairs={{0,1},{1,0},{2,3},{3,2},{4,5},{5,4},{6,7},{7,6},{8,9},{9,8},{10,11... | collective-permute-start | bytes 17694728 | tf_op jit(solution)/shard_map/ppermute | solution.py:378
  448.8 56.5 %collective-permute-start.19 = (f32[240,2560]{1,0:T(8,128)}, f32[240,2560]{1,0:T(8,128)}, u32[]{:S(2)}, u32[]{:S(2)}) collective-permute-start(f32[240,2560]{1,0:T(8,128)} %get-tuple-element.119), channel_id=1, source_target_pairs={{0,2},{1,3},{2,0},{3,1},{4,6},{5,7},{6,4},{7,5},{8,10},{9,11},{10,... | collective-permute-start | bytes 7372808 | tf_op jit(solution)/shard_map/ppermute | solution.py:384
  451.6 116.8 %collective-permute-start.21 = (f32[240,3072]{1,0:T(8,128)}, f32[240,3072]{1,0:T(8,128)S(1)}, u32[]{:S(2)}, u32[]{:S(2)}) collective-permute-start(f32[240,3072]{1,0:T(8,128)} %get-tuple-element.123), channel_id=1, source_target_pairs={{0,2},{1,3},{2,0},{3,1},{4,6},{5,7},{6,4},{7,5},{8,10},{9,11},{10,... | collective-permute-start | bytes 8847368 | tf_op jit(solution)/shard_map/ppermute | solution.py:384
  451.9 56.5 %collective-permute-start.20 = (f32[240,2560]{1,0:T(8,128)}, f32[240,2560]{1,0:T(8,128)}, u32[]{:S(2)}, u32[]{:S(2)}) collective-permute-start(f32[240,2560]{1,0:T(8,128)} %get-tuple-element.120), channel_id=1, source_target_pairs={{0,4},{1,5},{2,6},{3,7},{4,0},{5,1},{6,2},{7,3},{8,12},{9,13},{10,... | collective-permute-start | bytes 7372808 | tf_op jit(solution)/shard_map/ppermute | solution.py:385
  453.6 130.6 %collective-permute-start.22 = (f32[240,3072]{1,0:T(8,128)}, f32[240,3072]{1,0:T(8,128)}, u32[]{:S(2)}, u32[]{:S(2)}) collective-permute-start(f32[240,3072]{1,0:T(8,128)} %get-tuple-element.124), channel_id=1, source_target_pairs={{0,4},{1,5},{2,6},{3,7},{4,0},{5,1},{6,2},{7,3},{8,12},{9,13},{10,... | collective-permute-start | bytes 8847368 | tf_op jit(solution)/shard_map/ppermute | solution.py:385
  505.3 70.2 %collective-permute-start.14 = (f32[480,1024]{1,0:T(8,128)}, f32[480,1024]{1,0:T(8,128)}, u32[]{:S(2)}, u32[]{:S(2)}) collective-permute-start(f32[480,1024]{1,0:T(8,128)} %get-tuple-element.108), channel_id=1, source_target_pairs={{0,1},{1,0},{2,3},{3,2},{4,5},{5,4},{6,7},{7,6},{8,9},{9,8},{10,11... | collective-permute-start | bytes 5898248 | tf_op jit(solution)/shard_map/ppermute | solution.py:378
  508.5 146.6 %collective-permute-start.23 = (f32[240,2560]{1,0:T(8,128)}, f32[240,2560]{1,0:T(8,128)}, u32[]{:S(2)}, u32[]{:S(2)}) collective-permute-start(f32[240,2560]{1,0:T(8,128)} %get-tuple-element.127), channel_id=1, source_target_pairs={{0,2},{1,3},{2,0},{3,1},{4,6},{5,7},{6,4},{7,5},{8,10},{9,11},{10,... | collective-permute-start | bytes 7372808 | tf_op jit(solution)/shard_map/ppermute | solution.py:384
  568.4 88.2 %collective-permute-start.24 = (f32[240,2560]{1,0:T(8,128)}, f32[240,2560]{1,0:T(8,128)}, u32[]{:S(2)}, u32[]{:S(2)}) collective-permute-start(f32[240,2560]{1,0:T(8,128)} %get-tuple-element.128), channel_id=1, source_target_pairs={{0,4},{1,5},{2,6},{3,7},{4,0},{5,1},{6,2},{7,3},{8,12},{9,13},{10,... | collective-permute-start | bytes 7372808 | tf_op jit(solution)/shard_map/ppermute | solution.py:385
  575.4 212.5 %collective-permute-start.13 = (f32[1024,960]{0,1:T(8,128)}, f32[1024,960]{0,1:T(8,128)}, u32[]{:S(2)}, u32[]{:S(2)}) collective-permute-start(f32[1024,960]{0,1:T(8,128)} %copy.30), channel_id=1, source_target_pairs={{0,8},{8,0},{1,9},{9,1},{2,10},{10,2},{3,11},{11,3},{4,12},{12,4},... | collective-permute-start | bytes 11796488 | tf_op jit(solution)/shard_map/ppermute | solution.py:401
  641.1 68.8 %collective-permute-start.26 = (f32[240,1536]{1,0:T(8,128)}, f32[240,1536]{1,0:T(8,128)S(1)}, u32[]{:S(2)}, u32[]{:S(2)}) collective-permute-start(f32[240,1536]{1,0:T(8,128)} %get-tuple-element.133), channel_id=1, source_target_pairs={{0,2},{1,3},{2,0},{3,1},{4,6},{5,7},{6,4},{7,5},{8,10},{9,11},{10,... | collective-permute-start | bytes 4423688 | tf_op jit(solution)/shard_map/ppermute | solution.py:384
  707.0 69.6 %collective-permute-start.36 = (f32[120,3072]{1,0:T(8,128)}, f32[120,3072]{1,0:T(8,128)}, u32[]{:S(2)}, u32[]{:S(2)}) collective-permute-start(f32[120,3072]{1,0:T(8,128)} %get-tuple-element.146), channel_id=1, source_target_pairs={{0,4},{1,5},{2,6},{3,7},{4,0},{5,1},{6,2},{7,3},{8,12},{9,13},{10,... | collective-permute-start | bytes 4423688 | tf_op jit(solution)/shard_map/ppermute | solution.py:397
  708.5 68.5 %collective-permute-start.37 = (f32[120,3072]{1,0:T(8,128)}, f32[120,3072]{1,0:T(8,128)}, u32[]{:S(2)}, u32[]{:S(2)}) collective-permute-start(f32[120,3072]{1,0:T(8,128)} %get-tuple-element.147), channel_id=1, source_target_pairs={{0,2},{1,3},{2,0},{3,1},{4,6},{5,7},{6,4},{7,5},{8,10},{9,11},{10,... | collective-permute-start | bytes 4423688 | tf_op jit(solution)/shard_map/ppermute | solution.py:398
  709.8 57.5 %collective-permute-start.35 = (f32[120,2560]{1,0:T(8,128)}, f32[120,2560]{1,0:T(8,128)}, u32[]{:S(2)}, u32[]{:S(2)}) collective-permute-start(f32[120,2560]{1,0:T(8,128)} %get-tuple-element.145), channel_id=1, source_target_pairs={{0,2},{1,3},{2,0},{3,1},{4,6},{5,7},{6,4},{7,5},{8,10},{9,11},{10,... | collective-permute-start | bytes 3686408 | tf_op jit(solution)/shard_map/ppermute | solution.py:398
  732.9 66.3 %collective-permute-start.38 = (f32[120,2560]{1,0:T(8,128)}, f32[120,2560]{1,0:T(8,128)}, u32[]{:S(2)}, u32[]{:S(2)}) collective-permute-start(f32[120,2560]{1,0:T(8,128)} %get-tuple-element.148), channel_id=1, source_target_pairs={{0,4},{1,5},{2,6},{3,7},{4,0},{5,1},{6,2},{7,3},{8,12},{9,13},{10,... | collective-permute-start | bytes 3686408 | tf_op jit(solution)/shard_map/ppermute | solution.py:397
  767.3 55.5 %collective-permute-start.39 = (f32[120,2560]{1,0:T(8,128)}, f32[120,2560]{1,0:T(8,128)S(1)}, u32[]{:S(2)}, u32[]{:S(2)}) collective-permute-start(f32[120,2560]{1,0:T(8,128)} %get-tuple-element.149), channel_id=1, source_target_pairs={{0,2},{1,3},{2,0},{3,1},{4,6},{5,7},{6,4},{7,5},{8,10},{9,11},{10,... | collective-permute-start | bytes 3686408 | tf_op jit(solution)/shard_map/ppermute | solution.py:398
  776.5 60.8 %collective-permute-start.42 = (f32[120,512]{1,0:T(8,128)}, f32[120,512]{1,0:T(8,128)}, u32[]{:S(2)}, u32[]{:S(2)}) collective-permute-start(f32[120,512]{1,0:T(8,128)} %get-tuple-element.152), channel_id=1, source_target_pairs={{0,4},{1,5},{2,6},{3,7},{4,0},{5,1},{6,2},{7,3},{8,12},{9,13},{10,... | collective-permute-start | bytes 737288 | tf_op jit(solution)/shard_map/ppermute | solution.py:397
  (50 other events, 999.8 us)

commit v2 on v1

--- a/solution.py
+++ b/solution.py
@@ -15,7 +15,7 @@
 STRIP = 256
 SUB = 16
 LANES = 128
-CHUNK_TILES = (2, 6, 10, 12, 10, 6, 2)
+CHUNK_TILES = (2, 2, 4, 8, 10, 10, 8, 4)
 LOWEST = -3.0e38
 VMEM_LIMIT = 60 * 1024 * 1024
 
@@ -29,7 +29,7 @@
     return pltpu.CompilerParams(dimension_semantics=("arbitrary",), vmem_limit_bytes=VMEM_LIMIT)
 
 
-def stats_kernel(steps, g_ref, e_ref, t_ref, out_ref, m_ref, zs_ref, zt_ref, kl_ref):
+def stats_kernel(steps, g_ref, e_ref, t_ref, out_ref, u_ref, m_ref, zs_ref, zt_ref, kl_ref):
     step = pl.program_id(0)
 
     @pl.when(step == 0)
@@ -63,6 +63,7 @@
             kl = kl_ref[rows, :] * decay
             for k, part in enumerate(parts):
                 tanh_val = jnp.tanh(block[:, k * LANES:(k + 1) * LANES] * (1.0 / SOFT_CAP))
+                u_ref[rows, k * LANES:(k + 1) * LANES] = tanh_val
                 zs = zs + jnp.exp2(tanh_val * (SOFT_CAP * LOG2E))
                 ex = jnp.exp2((part - top) * LOG2E)
                 zt = zt + ex
@@ -94,62 +95,63 @@
         functools.partial(stats_kernel, steps),
         name="stats",
         grid=(steps,),
-        out_shape=jax.ShapeDtypeStruct((8, tokens), jnp.float32),
+        out_shape=[
+            jax.ShapeDtypeStruct((8, tokens), jnp.float32),
+            jax.ShapeDtypeStruct((tokens, vocab), jnp.float32),
+        ],
         in_specs=[
             pl.BlockSpec((tokens, dim), lambda j: (0, 0)),
             pl.BlockSpec((dim, TILE), lambda j: (0, j)),
             pl.BlockSpec((tokens, TILE), lambda j: (0, j)),
         ],
-        out_specs=pl.BlockSpec((8, tokens), lambda j: (0, 0)),
+        out_specs=[
+            pl.BlockSpec((8, tokens), lambda j: (0, 0)),
+            pl.BlockSpec((tokens, TILE), lambda j: (0, j)),
+        ],
         scratch_shapes=[pltpu.VMEM((tokens, LANES), jnp.float32)] * 4,
         compiler_params=params(),
-        cost_estimate=pl.CostEstimate(flops=2 * tokens * dim * vocab, bytes_accessed=2 * vocab * (tokens + dim), transcendentals=3 * tokens * vocab),
+        cost_estimate=pl.CostEstimate(flops=2 * tokens * dim * vocab, bytes_accessed=2 * vocab * (3 * tokens + dim), transcendentals=3 * tokens * vocab),
     )(normed, emb_t, teach)
 
 
-def a_kernel(order_ref, prev_ref, coef_ref, g_ref, gp_ref, e_ref, t_ref, dr_ref, pp_ref, dg_ref, tok_ref):
+def a_kernel(chained, *refs):
+    if chained:
+        order_ref, prev_ref, *refs = refs
+    coef_ref, gp_ref, e_ref, t_ref, u_ref, dr_ref, pp_ref, dg_ref, tok_ref = refs
+
     @pl.when(pl.program_id(0) == 0)
     def _():
-        dg_ref[...] = prev_ref[...]
+        dg_ref[...] = prev_ref[...] if chained else jnp.zeros_like(dg_ref)
         tok_ref[...] = jnp.zeros_like(tok_ref)
 
     groups = TILE // LANES
-    tokens = g_ref.shape[0]
-
-    def logits(strip):
-        return jnp.dot(g_ref[pl.ds(strip * STRIP, STRIP), :], e_ref[...], preferred_element_type=jnp.float32)
-
-    raw = logits(0)
+    tokens = u_ref.shape[0]
     for strip in range(tokens // STRIP):
-        following = logits(strip + 1) if (strip + 1) * STRIP < tokens else None
         for sub in range(STRIP // SUB):
             rows = pl.ds(strip * STRIP + sub * SUB, SUB)
-            block = raw[sub * SUB:(sub + 1) * SUB]
-            tea = t_ref[rows, :].astype(jnp.float32)
             top = coef_ref[0, rows, :]
             stu_w = coef_ref[1, rows, :]
             tea_w = coef_ref[2, rows, :]
             for k in range(groups):
                 cols = slice(k * LANES, (k + 1) * LANES)
-                tanh_val = jnp.tanh(block[:, cols] * (1.0 / SOFT_CAP))
+                tanh_val = u_ref[rows, cols]
                 stu = jnp.exp2(tanh_val * (SOFT_CAP * LOG2E)) * stu_w
-                soft = jnp.exp2((tea[:, cols] - top) * LOG2E) * tea_w
+                soft = jnp.exp2((t_ref[rows, cols].astype(jnp.float32) - top) * LOG2E) * tea_w
                 d_raw = (stu - soft) * (1.0 - tanh_val * tanh_val)
                 dr_ref[rows, cols] = d_raw.astype(jnp.bfloat16)
-        raw = following
-
-    d_raw = dr_ref[...]
-    pp_ref[...] = jnp.dot(gp_ref[0], d_raw, preferred_element_type=jnp.float32)
-    dg_ref[...] += lax.dot_general(d_raw, e_ref[...], (((1,), (1,)), ((), ())), preferred_element_type=jnp.float32)
-
-
-def run_a(first, tiles, order, prev, coef, normed, g_partner, emb_t, teach):
-    tokens, dim = normed.shape
+        part = pl.ds(strip * STRIP, STRIP)
+        dg_ref[part, :] += lax.dot_general(dr_ref[part, :], e_ref[...], (((1,), (1,)), ((), ())), preferred_element_type=jnp.float32)
+    pp_ref[...] = jnp.dot(gp_ref[0], dr_ref[...], preferred_element_type=jnp.float32)
+
+
+def run_a(first, tiles, chain, coef, g_partner, emb_t, teach, tanh_all):
+    tokens = teach.shape[0]
+    dim = emb_t.shape[0]
     half = tiles // 2
     width = tiles * TILE
     rows = g_partner.shape[1]
     return pl.pallas_call(
-        a_kernel,
+        functools.partial(a_kernel, bool(chain)),
         name="dlogits",
         grid=(tiles,),
         out_shape=[
@@ -161,10 +163,11 @@
         in_specs=[
             pl.BlockSpec((8, LANES), lambda j: (0, 0)),
             pl.BlockSpec((tokens, dim), lambda j: (0, 0)),
+        ][:len(chain)] + [
             pl.BlockSpec((3, tokens, LANES), lambda j: (0, 0, 0)),
-            pl.BlockSpec((tokens, dim), lambda j: (0, 0)),
             pl.BlockSpec((1, rows, tokens), lambda j: (j // half, 0, 0)),
             pl.BlockSpec((dim, TILE), lambda j: (0, first + j)),
+            pl.BlockSpec((tokens, TILE), lambda j: (0, first + j)),
             pl.BlockSpec((tokens, TILE), lambda j: (0, first + j)),
         ],
         out_specs=[
@@ -174,8 +177,8 @@
             pl.BlockSpec((8, LANES), lambda j: (0, 0)),
         ],
         compiler_params=params(),
-        cost_estimate=pl.CostEstimate(flops=5 * tokens * dim * width, bytes_accessed=10 * tokens * width, transcendentals=3 * tokens * width),
-    )(order, prev, coef, normed, g_partner, emb_t, teach)
+        cost_estimate=pl.CostEstimate(flops=4 * tokens * dim * width, bytes_accessed=12 * tokens * width, transcendentals=2 * tokens * width),
+    )(*chain, coef, g_partner, emb_t, teach, tanh_all)
 
 
 def b_kernel(half, order_ref, go_ref, dr_ref, r_ref, keep_ref, send0_ref, send1_ref, tok_ref):
@@ -325,6 +328,18 @@
     )(*operands)
 
 
+def plan():
+    chunks = len(CHUNK_TILES)
+    steps = [("dlog", 0), ("own", 0), ("dlog", 1), ("own", 1)]
+    for k in range(2, chunks):
+        steps.append(("dlog", k))
+        if k >= 3:
+            steps.append(("own", k - 1))
+            steps.append(("relay", k - 3))
+    steps.append(("own", chunks - 1))
+    return steps + [("relay", k) for k in range(chunks - 3, chunks)]
+
+
 def solution(mesh):
     dp = mesh.shape['dp']
     swap = {bit: [(i, i ^ bit) for i in range(dp)] for bit in range(1, dp)}
@@ -344,7 +359,7 @@
         normed_f32, norm_pull = jax.vjp(rms_norm, hid_loc.astype(jnp.float32), norm_w.astype(jnp.float32))
         normed = normed_f32.astype(jnp.bfloat16)
         emb_t = emb_loc.T
-        mine = run_stats(normed, emb_t, teach_loc)
+        mine, tanh_all = run_stats(normed, emb_t, teach_loc)
 
         blocks = normed.T.reshape(dp, dim // dp, tokens)
 
@@ -365,38 +380,30 @@
         coef = jnp.stack([top, weight / sum_stu, weight / sum_tea])
         coef = jnp.broadcast_to(coef[:, :, None], (3, tokens, LANES))
 
-        zero_token = jnp.zeros((8, LANES), jnp.float32)
-        grad_part = jnp.zeros((tokens, dim), jnp.float32)
         count_chunks = len(CHUNK_TILES)
         firsts = [sum(CHUNK_TILES[:k]) for k in range(count_chunks)]
-        a_token, b_token = {}, {}
+        last = None
+        grad_part = None
         d_raw, recv, state = {}, {}, {}
-
-        def do_a(k, grad):
-            order = b_token[k - 2] if k >= 2 else zero_token
-            d_raw[k], part, grad, a_token[k] = run_a(firsts[k], CHUNK_TILES[k], order, grad, coef, normed, g_partner, emb_t, teach_loc)
-            recv[k] = lax.ppermute(part, 'dp', swap[1])
-            return grad
-
-        def do_b(k):
-            order = a_token[min(k + 1, count_chunks - 1)]
-            keep, send0, send1, b_token[k] = run_b(CHUNK_TILES[k], order, g_own, d_raw[k], recv[k])
-            rx = lax.ppermute(send0, 'dp', swap[2])
-            ry = lax.ppermute(send1, 'dp', swap[4])
-            state[k] = (keep, rx, ry)
-
-        grad_part = do_a(0, grad_part)
-        for k in range(1, count_chunks):
-            grad_part = do_a(k, grad_part)
-            do_b(k - 1)
-        do_b(count_chunks - 1)
-
-        order = b_token[count_chunks - 1]
-        for k in range(count_chunks):
-            last0, last1, order = run_relay(CHUNK_TILES[k], order, *state[k])
-            last0 = lax.ppermute(last0, 'dp', swap[4])
-            last1 = lax.ppermute(last1, 'dp', swap[2])
-            state[k] += (last0, last1)
+        for verb, k in plan():
+            tiles = CHUNK_TILES[k]
+            if verb == "dlog":
+                chain = () if last is None else (last, grad_part)
+                d_raw[k], part, grad_part, last = run_a(firsts[k], tiles, chain, coef, g_partner, emb_t, teach_loc, tanh_all)
+            elif verb == "own":
+                keep, send0, send1, last = run_b(tiles, last, g_own, d_raw[k], recv[k])
+            else:
+                last0, last1, last = run_relay(tiles, last, *state[k])
+            if verb == "dlog":
+                recv[k] = lax.ppermute(part, 'dp', swap[1])
+            elif verb == "own":
+                rx = lax.ppermute(send0, 'dp', swap[2])
+                ry = lax.ppermute(send1, 'dp', swap[4])
+                state[k] = (keep, rx, ry)
+            else:
+                last0 = lax.ppermute(last0, 'dp', swap[4])
+                last1 = lax.ppermute(last1, 'dp', swap[2])
+                state[k] += (last0, last1)
 
         grad_other = lax.ppermute(grad_part, 'tp', across)
         grad_normed = grad_part + grad_other
@@ -405,7 +412,7 @@
 
         grad_emb = None
         for k in range(count_chunks):
-            order = order if k < count_chunks - 3 else jnp.broadcast_to(grad_w[:LANES], (8, LANES))
+            order = last if k < count_chunks - 3 else jnp.broadcast_to(grad_w[:LANES], (8, LANES))
             grad_emb = run_final(firsts[k], CHUNK_TILES[k], vocab, order, grad_emb, *state[k])
         return loss_val, grad_hid.astype(jnp.bfloat16), grad_emb.T, grad_w
 

time: 850 us -> 824 us (0.969)
  Pallas kernels: 488 us -> 447 us
  blocking collectives: 16.1 us -> 46.4 us
  waiting for transfers between devices: 236 us -> 212 us
    ppermute x21 -> x24, waiting for transfers between devices: 138 us -> 66 us  [the longest x8 30.1 us: device_fn(): rx = lax.ppermute(send0, 'dp', swap[2])]
    pallas_call x7 -> x8, Pallas kernels: 225 us -> 171 us  [run_a(): pl.pallas_call(functools.partial(a_kernel, bool(chain)), name='dlogits',...]
    psum x1, blocking collectives: 16.1 us -> 46.4 us  [device_fn(): loss_val, grad_w = lax.psum((jnp.sum(weight * kl_tok), grad_scale), 'dp')]
    ppermute x7 -> x8, waiting for transfers between devices: 78.7 us -> 104 us  [device_fn(): last0 = lax.ppermute(last0, 'dp', swap[4])]
    ppermute x7 -> x8, waiting for transfers between devices: 18.5 us -> 41.3 us  [device_fn(): last1 = lax.ppermute(last1, 'dp', swap[2])]
    pallas_call x7 -> x8, Pallas kernels: 83.1 us -> 85.2 us  [run_b(): pl.pallas_call(functools.partial(b_kernel, half), name='own_half', grid=(...]
    pallas_call x7 -> x8, Pallas kernels: 38.8 us -> 40.5 us  [run_relay(): pl.pallas_call(functools.partial(relay_kernel, half), name='relay', grid=...]
    pallas_call x7 -> x8, Pallas kernels: 40.7 us -> 42.2 us  [run_final(): pl.pallas_call(body, name='finish', grid=(tiles,), out_shape=jax.ShapeDty...]
  transfers between devices with their start and end apart: 44 -> 49, of which waited for: 11 -> 16; matrix products, arithmetic and copies ran while one was open for 5% -> 5% of each run, Pallas kernels for 56% -> 49%
where the time goes in v2:
time: 824 us; the launch traced here: 811 us
  Pallas kernels  447 us (54%)
  waiting for transfers between devices  212 us (26%)
  starting transfers between devices  47.5 us (6%)
  blocking collectives  46.4 us (6%)
  local copies, waits for them, and re-layouts  33.5 us (4%)
  other arithmetic  22.2 us (3%)
    pallas_call x8, Pallas kernels, run_a(): pl.pallas_call(functools.partial(a_kernel, bool(chain)), name='dlogits',...  171 us
    pallas_call x1, Pallas kernels, run_stats(): pl.pallas_call(functools.partial(stats_kernel, steps), name='stats', grid...  108 us
    ppermute x8, waiting for transfers between devices, device_fn(): last0 = lax.ppermute(last0, 'dp', swap[4])  104 us
    pallas_call x8, Pallas kernels, run_b(): pl.pallas_call(functools.partial(b_kernel, half), name='own_half', grid=(...  85.2 us
    psum x1, blocking collectives, device_fn(): loss_val, grad_w = lax.psum((jnp.sum(weight * kl_tok), grad_scale), 'dp')  46.4 us
    pallas_call x8, Pallas kernels, run_final(): pl.pallas_call(body, name='finish', grid=(tiles,), out_shape=jax.ShapeDty...  42.2 us
    ppermute x8, waiting for transfers between devices, device_fn(): last1 = lax.ppermute(last1, 'dp', swap[2])  41.3 us
    pallas_call x8, Pallas kernels, run_relay(): pl.pallas_call(functools.partial(relay_kernel, half), name='relay', grid=...  40.5 us
  transfers between devices with their start and end apart: 49, of which 16 were waited for; matrix products, arithmetic and copies ran while one was open for 5% of the time, Pallas kernels for 49%

profile of v2, /device:TPU:0, one launch (start us, length us, event | category | flops | bytes accessed | tf_op | source)
XLA Modules:
  0.0 810.7 jit_solution(6227325357783334381)
XLA Ops:
  21.8 108.3 %stats.1 = (f32[8,1024]{1,0:T(8,128)}, f32[1024,24576]{1,0:T(8,128)}) custom-call(bf16[1024,960]{1,0:T(8,128)(2,1)} %fusion.2.g_ref, bf16[960,24576]{1,0:T(8,128)(2,1)} %bitcast.40, bf16[1024,24576]{1,0:T(8,128)(2,1)} %refs_5_.13), custom_call_target="tpu_custom_call" | custom-call | flops 48318382080 | bytes 198180864 | tf_op jit(solution)/shard_map/stats/pallas_call | solution.py:94
  140.3 9.9 %dlogits.8 = (bf16[1024,1024]{1,0:T(8,128)(2,1)}, f32[480,1024]{1,0:T(8,128)}, f32[1024,960]{1,0:T(8,128)}, f32[8,128]{1,0:T(8,128)}) custom-call(f32[3,1024,128]{2,1,0:T(8,128)} %broadcast_in_dim.9.refs_0_.refs_2_, bf16[2,480,1024]{2,1,0:T(8,128)(2,1)} %pad_maximum_fusion.refs_1_.refs_3_, bf16[960,24576]{1,0:T(8,128)(2,1)} %bitcast.41, ...), custom_call_target="tpu_custom_call" | custom-call | flops 4026531840 | bytes 12582912 | tf_op jit(solution)/shard_map/dlogits/pallas_call | solution.py:153
  160.6 11.4 %dlogits.9 = (bf16[1024,1024]{1,0:T(8,128)(2,1)}, f32[480,1024]{1,0:T(8,128)}, f32[1024,960]{1,0:T(8,128)}, f32[8,128]{1,0:T(8,128)}) custom-call(f32[8,128]{1,0:T(8,128)} %get-tuple-element.99.refs_0_, f32[1024,960]{1,0:T(8,128)} %get-tuple-element.100.refs_1_, f32[3,1024,128]{2,1,0:T(8,128)} %broadcast_in_dim.9.refs_0_.refs_2_, ...), custom_call_target="tpu_custom_call" | custom-call | flops 4026531840 | bytes 12582912 | tf_op jit(solution)/shard_map/dlogits/pallas_call | solution.py:153
  182.2 17.1 %dlogits.10 = (bf16[1024,2048]{1,0:T(8,128)(2,1)}, f32[480,2048]{1,0:T(8,128)}, f32[1024,960]{1,0:T(8,128)}, f32[8,128]{1,0:T(8,128)}) custom-call(f32[8,128]{1,0:T(8,128)} %get-tuple-element.104.refs_0_, f32[1024,960]{1,0:T(8,128)} %get-tuple-element.105.refs_1_, f32[3,1024,128]{2,1,0:T(8,128)} %broadcast_in_dim.9.refs_0_.refs_2_, ...), custom_call_target="tpu_custom_call" | custom-call | flops 8053063680 | bytes 25165824 | tf_op jit(solution)/shard_map/dlogits/pallas_call | solution.py:153
  199.5 26.3 %dlogits.11 = (bf16[1024,4096]{1,0:T(8,128)(2,1)}, f32[480,4096]{1,0:T(8,128)}, f32[1024,960]{1,0:T(8,128)}, f32[8,128]{1,0:T(8,128)}) custom-call(f32[8,128]{1,0:T(8,128)} %get-tuple-element.106.refs_0_, f32[1024,960]{1,0:T(8,128)} %get-tuple-element.107.refs_1_, f32[3,1024,128]{2,1,0:T(8,128)} %broadcast_in_dim.9.refs_0_.refs_2_, ...), custom_call_target="tpu_custom_call" | custom-call | flops 16106127360 | bytes 50331648 | tf_op jit(solution)/shard_map/dlogits/pallas_call | solution.py:153
  231.3 7.7 own_half.10
  243.4 31.4 %dlogits.12 = (bf16[1024,5120]{1,0:T(8,128)(2,1)}, f32[480,5120]{1,0:T(8,128)}, f32[1024,960]{1,0:T(8,128)}, f32[8,128]{1,0:T(8,128)}) custom-call(f32[8,128]{1,0:T(8,128)} %get-tuple-element.115.refs_0_, f32[1024,960]{1,0:T(8,128)} %get-tuple-element.116.refs_1_, f32[3,1024,128]{2,1,0:T(8,128)} %broadcast_in_dim.9.refs_0_.refs_2_, ...), custom_call_target="tpu_custom_call" | custom-call | flops 20132659200 | bytes 62914560 | tf_op jit(solution)/shard_map/dlogits/pallas_call | solution.py:153
  276.9 13.7 %own_half.11 = (f32[240,4096]{1,0:T(8,128)}, f32[240,2048]{1,0:T(8,128)}, f32[240,2048]{1,0:T(8,128)}, f32[8,128]{1,0:T(8,128)}) custom-call(f32[8,128]{1,0:T(8,128)} %get-tuple-element.117.order_ref, bf16[2,480,1024]{2,1,0:T(8,128)(2,1)} %pad_maximum_fusion.1.go_ref, bf16[1024,4096]{1,0:T(8,128)(2,1)} %get-tuple-element.118.dr_ref, ...), custom_call_target="tpu_custom_call" | custom-call | flops 4026531840 | bytes 24117248 | tf_op jit(solution)/shard_map/own_half/pallas_call | solution.py:210
  293.7 31.5 %dlogits.13 = (bf16[1024,5120]{1,0:T(8,128)(2,1)}, f32[480,5120]{1,0:T(8,128)}, f32[1024,960]{1,0:T(8,128)}, f32[8,128]{1,0:T(8,128)}) custom-call(f32[8,128]{1,0:T(8,128)} %get-tuple-element.124.refs_0_, f32[1024,960]{1,0:T(8,128)} %get-tuple-element.125.refs_1_, f32[3,1024,128]{2,1,0:T(8,128)} %broadcast_in_dim.9.refs_0_.refs_2_, ...), custom_call_target="tpu_custom_call" | custom-call | flops 20132659200 | bytes 62914560 | tf_op jit(solution)/shard_map/dlogits/pallas_call | solution.py:153
  327.2 16.4 %own_half.12 = (f32[240,5120]{1,0:T(8,128)}, f32[240,2560]{1,0:T(8,128)}, f32[240,2560]{1,0:T(8,128)}, f32[8,128]{1,0:T(8,128)}) custom-call(f32[8,128]{1,0:T(8,128)} %get-tuple-element.126.order_ref, bf16[2,480,1024]{2,1,0:T(8,128)(2,1)} %pad_maximum_fusion.1.go_ref, bf16[1024,5120]{1,0:T(8,128)(2,1)} %get-tuple-element.127.dr_ref, ...), custom_call_target="tpu_custom_call" | custom-call | flops 5033164800 | bytes 30146560 | tf_op jit(solution)/shard_map/own_half/pallas_call | solution.py:210
  355.4 26.8 %dlogits.14 = (bf16[1024,4096]{1,0:T(8,128)(2,1)}, f32[480,4096]{1,0:T(8,128)}, f32[1024,960]{1,0:T(8,128)}, f32[8,128]{1,0:T(8,128)}) custom-call(f32[8,128]{1,0:T(8,128)} %get-tuple-element.133.refs_0_, f32[1024,960]{1,0:T(8,128)} %get-tuple-element.134.refs_1_, f32[3,1024,128]{2,1,0:T(8,128)} %broadcast_in_dim.9.refs_0_.refs_2_, ...), custom_call_target="tpu_custom_call" | custom-call | flops 16106127360 | bytes 50331648 | tf_op jit(solution)/shard_map/dlogits/pallas_call | solution.py:153
  384.9 48.4 %collective-permute-done.33.last0_ref = f32[120,512]{1,0:T(8,128)S(1)} collective-permute-done((f32[120,512]{1,0:T(8,128)S(1)}, f32[120,512]{1,0:T(8,128)S(1)}, u32[]{:S(2)}, u32[]{:S(2)}) %collective-permute-start.33) | collective-permute-done | bytes 245792 | tf_op jit(solution)/shard_map/ppermute | solution.py:404
  445.3 16.3 %own_half.13 = (f32[240,5120]{1,0:T(8,128)}, f32[240,2560]{1,0:T(8,128)}, f32[240,2560]{1,0:T(8,128)}, f32[8,128]{1,0:T(8,128)}) custom-call(f32[8,128]{1,0:T(8,128)} %get-tuple-element.135.order_ref, bf16[2,480,1024]{2,1,0:T(8,128)(2,1)} %pad_maximum_fusion.1.go_ref, bf16[1024,5120]{1,0:T(8,128)(2,1)} %get-tuple-element.136.dr_ref, ...), custom_call_target="tpu_custom_call" | custom-call | flops 5033164800 | bytes 30146560 | tf_op jit(solution)/shard_map/own_half/pallas_call | solution.py:210
  468.0 33.5 %collective-permute-done.35.last0_ref = f32[120,512]{1,0:T(8,128)S(1)} collective-permute-done((f32[120,512]{1,0:T(8,128)S(1)}, f32[120,512]{1,0:T(8,128)S(1)}, u32[]{:S(2)}, u32[]{:S(2)}) %collective-permute-start.35) | collective-permute-done | bytes 245792 | tf_op jit(solution)/shard_map/ppermute | solution.py:404
  502.7 16.6 %dlogits.15 = (bf16[1024,2048]{1,0:T(8,128)(2,1)}, f32[480,2048]{1,0:T(8,128)}, f32[1024,960]{1,0:T(8,128)}, f32[8,128]{1,0:T(8,128)}) custom-call(f32[8,128]{1,0:T(8,128)} %get-tuple-element.142.refs_0_, f32[1024,960]{1,0:T(8,128)} %get-tuple-element.143.refs_1_, f32[3,1024,128]{2,1,0:T(8,128)} %broadcast_in_dim.9.refs_0_.refs_2_, ...), custom_call_target="tpu_custom_call" | custom-call | flops 8053063680 | bytes 25165824 | tf_op jit(solution)/shard_map/dlogits/pallas_call | solution.py:153
  529.3 22.4 %collective-permute-done.39.last0_ref = f32[120,2048]{1,0:T(8,128)} collective-permute-done((f32[120,2048]{1,0:T(8,128)}, f32[120,2048]{1,0:T(8,128)}, u32[]{:S(2)}, u32[]{:S(2)}) %collective-permute-start.39) | collective-permute-done | bytes 983072 | tf_op jit(solution)/shard_map/ppermute | solution.py:404
  553.8 13.8 %own_half.14 = (f32[240,4096]{1,0:T(8,128)}, f32[240,2048]{1,0:T(8,128)}, f32[240,2048]{1,0:T(8,128)}, f32[8,128]{1,0:T(8,128)}) custom-call(f32[8,128]{1,0:T(8,128)} %get-tuple-element.145.order_ref, bf16[2,480,1024]{2,1,0:T(8,128)(2,1)} %pad_maximum_fusion.1.go_ref, bf16[1024,4096]{1,0:T(8,128)(2,1)} %get-tuple-element.146.dr_ref, ...), custom_call_target="tpu_custom_call" | custom-call | flops 4026531840 | bytes 24117248 | tf_op jit(solution)/shard_map/own_half/pallas_call | solution.py:210
  567.6 35.5 %collective-permute-done.40.last1_ref = f32[120,2048]{1,0:T(8,128)S(1)} collective-permute-done((f32[120,2048]{1,0:T(8,128)}, f32[120,2048]{1,0:T(8,128)S(1)}, u32[]{:S(2)}, u32[]{:S(2)}) %collective-permute-start.40) | collective-permute-done | bytes 983072 | tf_op jit(solution)/shard_map/ppermute | solution.py:405
  614.2 7.7 own_half.15
  631.7 17.4 %collective-permute-done.29.rx_ref = f32[240,2048]{1,0:T(8,128)} collective-permute-done((f32[240,2048]{1,0:T(8,128)}, f32[240,2048]{1,0:T(8,128)}, u32[]{:S(2)}, u32[]{:S(2)}) %collective-permute-start.29) | collective-permute-done | bytes 1966112 | tf_op jit(solution)/shard_map/ppermute | solution.py:400
  671.5 26.4 %collective-permute-done.32.ry_ref = f32[240,1024]{1,0:T(8,128)} collective-permute-done((f32[240,1024]{1,0:T(8,128)}, f32[240,1024]{1,0:T(8,128)}, u32[]{:S(2)}, u32[]{:S(2)}) %collective-permute-start.32) | collective-permute-done | bytes 983072 | tf_op jit(solution)/shard_map/ppermute | solution.py:401
  705.1 46.4 %all-reduce = (f32[]{:T(128)}, f32[960]{0:T(1024)S(1)}) all-reduce(f32[]{:T(128)} %get-tuple-element.222, f32[960]{0:T(1024)S(1)} %get-tuple-element.196), channel_id=1, replica_groups=mesh['tp'=2,'dp'=8] {'dp'}, use_global_device_ids=true, to_apply=%region_3.4 | all-reduce | flops 961 | bytes 7688 | tf_op jit(solution)/shard_map/psum | solution.py:411
  781.4 8.0 finish.12.buf_ref
  790.0 8.0 finish.13.buf_ref
  (210 shorter events, 208.5 us)
Async XLA Ops:
  2.6 128.2 %collective-permute-start.5 = (f32[8,128]{1,0:T(8,128)S(1)}, f32[8,128]{1,0:T(8,128)S(1)}, u32[]{:S(2)}, u32[]{:S(2)}) collective-permute-start(f32[8,128]{1,0:T(8,128)S(1)} %broadcast_in_dim.8), channel_id=1, source_target_pairs={{0,6},{1,7},{2,4},{3,5},{4,2},{5,3},{6,0},{7,1},{8,14},{9,15},{10,... | collective-permute-start | bytes 12296 | tf_op jit(solution)/shard_map/ppermute | solution.py:356
  6.8 124.1 %collective-permute-start.4 = (f32[8,128]{1,0:T(8,128)S(1)}, f32[8,128]{1,0:T(8,128)S(1)}, u32[]{:S(2)}, u32[]{:S(2)}) collective-permute-start(f32[8,128]{1,0:T(8,128)S(1)} %broadcast_in_dim.8), channel_id=1, source_target_pairs={{0,5},{1,4},{2,7},{3,6},{4,1},{5,0},{6,3},{7,2},{8,13},{9,12},{10,... | collective-permute-start | bytes 12296 | tf_op jit(solution)/shard_map/ppermute | solution.py:356
  6.8 125.9 %collective-permute-start.3 = (f32[8,128]{1,0:T(8,128)S(1)}, f32[8,128]{1,0:T(8,128)S(1)}, u32[]{:S(2)}, u32[]{:S(2)}) collective-permute-start(f32[8,128]{1,0:T(8,128)S(1)} %broadcast_in_dim.8), channel_id=1, source_target_pairs={{0,4},{1,5},{2,6},{3,7},{4,0},{5,1},{6,2},{7,3},{8,12},{9,13},{10,... | collective-permute-start | bytes 12296 | tf_op jit(solution)/shard_map/ppermute | solution.py:356
  7.9 126.5 %collective-permute-start.2 = (f32[8,128]{1,0:T(8,128)S(1)}, f32[8,128]{1,0:T(8,128)S(1)}, u32[]{:S(2)}, u32[]{:S(2)}) collective-permute-start(f32[8,128]{1,0:T(8,128)S(1)} %broadcast_in_dim.8), channel_id=1, source_target_pairs={{0,3},{1,2},{2,1},{3,0},{4,7},{5,6},{6,5},{7,4},{8,11},{9,10},{10,... | collective-permute-start | bytes 12296 | tf_op jit(solution)/shard_map/ppermute | solution.py:356
  8.8 125.7 %collective-permute-start.1 = (f32[8,128]{1,0:T(8,128)S(1)}, f32[8,128]{1,0:T(8,128)S(1)}, u32[]{:S(2)}, u32[]{:S(2)}) collective-permute-start(f32[8,128]{1,0:T(8,128)S(1)} %broadcast_in_dim.8), channel_id=1, source_target_pairs={{0,2},{1,3},{2,0},{3,1},{4,6},{5,7},{6,4},{7,5},{8,10},{9,11},{10,... | collective-permute-start | bytes 12296 | tf_op jit(solution)/shard_map/ppermute | solution.py:356
  325.2 119.5 %collective-permute-start.19 = (f32[480,5120]{1,0:T(8,128)}, f32[480,5120]{1,0:T(8,128)}, u32[]{:S(2)}, u32[]{:S(2)}) collective-permute-start(f32[480,5120]{1,0:T(8,128)} %get-tuple-element.137), channel_id=1, source_target_pairs={{0,1},{1,0},{2,3},{3,2},{4,5},{5,4},{6,7},{7,6},{8,9},{9,8},{10,11... | collective-permute-start | bytes 29491208 | tf_op jit(solution)/shard_map/ppermute | solution.py:398
  382.2 171.0 %collective-permute-start.23 = (f32[480,4096]{1,0:T(8,128)}, f32[480,4096]{1,0:T(8,128)}, u32[]{:S(2)}, u32[]{:S(2)}) collective-permute-start(f32[480,4096]{1,0:T(8,128)} %get-tuple-element.147), channel_id=1, source_target_pairs={{0,1},{1,0},{2,3},{3,2},{4,5},{5,4},{6,7},{7,6},{8,9},{9,8},{10,11... | collective-permute-start | bytes 23592968 | tf_op jit(solution)/shard_map/ppermute | solution.py:398
  382.3 60.3 %collective-permute-start.20 = (f32[240,2048]{1,0:T(8,128)}, f32[240,2048]{1,0:T(8,128)}, u32[]{:S(2)}, u32[]{:S(2)}) collective-permute-start(f32[240,2048]{1,0:T(8,128)} %get-tuple-element.140), channel_id=1, source_target_pairs={{0,2},{1,3},{2,0},{3,1},{4,6},{5,7},{6,4},{7,5},{8,10},{9,11},{10,... | collective-permute-start | bytes 5898248 | tf_op jit(solution)/shard_map/ppermute | solution.py:400
  382.9 60.2 %collective-permute-start.21 = (f32[240,2048]{1,0:T(8,128)}, f32[240,2048]{1,0:T(8,128)}, u32[]{:S(2)}, u32[]{:S(2)}) collective-permute-start(f32[240,2048]{1,0:T(8,128)} %get-tuple-element.141), channel_id=1, source_target_pairs={{0,4},{1,5},{2,6},{3,7},{4,0},{5,1},{6,2},{7,3},{8,12},{9,13},{10,... | collective-permute-start | bytes 5898248 | tf_op jit(solution)/shard_map/ppermute | solution.py:401
  441.2 85.2 %collective-permute-start.24 = (f32[240,2560]{1,0:T(8,128)}, f32[240,2560]{1,0:T(8,128)S(1)}, u32[]{:S(2)}, u32[]{:S(2)}) collective-permute-start(f32[240,2560]{1,0:T(8,128)} %get-tuple-element.150), channel_id=1, source_target_pairs={{0,2},{1,3},{2,0},{3,1},{4,6},{5,7},{6,4},{7,5},{8,10},{9,11},{10,... | collective-permute-start | bytes 7372808 | tf_op jit(solution)/shard_map/ppermute | solution.py:400
  442.6 85.1 %collective-permute-start.25 = (f32[240,2560]{1,0:T(8,128)}, f32[240,2560]{1,0:T(8,128)}, u32[]{:S(2)}, u32[]{:S(2)}) collective-permute-start(f32[240,2560]{1,0:T(8,128)} %get-tuple-element.151), channel_id=1, source_target_pairs={{0,4},{1,5},{2,6},{3,7},{4,0},{5,1},{6,2},{7,3},{8,12},{9,13},{10,... | collective-permute-start | bytes 7372808 | tf_op jit(solution)/shard_map/ppermute | solution.py:401
  443.1 58.4 %collective-permute-start.35 = (f32[120,512]{1,0:T(8,128)S(1)}, f32[120,512]{1,0:T(8,128)S(1)}, u32[]{:S(2)}, u32[]{:S(2)}) collective-permute-start(f32[120,512]{1,0:T(8,128)S(1)} %copy-done.33), channel_id=1, source_target_pairs={{0,4},{1,5},{2,6},{3,7},{4,0},{5,1},{6,2},{7,3},{8,12},{9,13},{10,... | collective-permute-start | bytes 737288 | tf_op jit(solution)/shard_map/ppermute | solution.py:404
  444.6 57.4 %collective-permute-start.36 = (f32[120,512]{1,0:T(8,128)S(1)}, f32[120,512]{1,0:T(8,128)S(1)}, u32[]{:S(2)}, u32[]{:S(2)}) collective-permute-start(f32[120,512]{1,0:T(8,128)S(1)} %copy-done.32), channel_id=1, source_target_pairs={{0,2},{1,3},{2,0},{3,1},{4,6},{5,7},{6,4},{7,5},{8,10},{9,11},{10,... | collective-permute-start | bytes 737288 | tf_op jit(solution)/shard_map/ppermute | solution.py:405
  519.3 94.4 %collective-permute-start.26 = (f32[480,2048]{1,0:T(8,128)}, f32[480,2048]{1,0:T(8,128)}, u32[]{:S(2)}, u32[]{:S(2)}) collective-permute-start(f32[480,2048]{1,0:T(8,128)} %get-tuple-element.154), channel_id=1, source_target_pairs={{0,1},{1,0},{2,3},{3,2},{4,5},{5,4},{6,7},{7,6},{8,9},{9,8},{10,11... | collective-permute-start | bytes 11796488 | tf_op jit(solution)/shard_map/ppermute | solution.py:398
  524.8 97.8 %collective-permute-start.22 = (f32[1024,960]{0,1:T(8,128)}, f32[1024,960]{0,1:T(8,128)}, u32[]{:S(2)}, u32[]{:S(2)}) collective-permute-start(f32[1024,960]{0,1:T(8,128)} %copy.31), channel_id=1, source_target_pairs={{0,8},{8,0},{1,9},{9,1},{2,10},{10,2},{3,11},{11,3},{4,12},{12,4},... | collective-permute-start | bytes 11796488 | tf_op jit(solution)/shard_map/ppermute | solution.py:408
  526.4 78.1 %collective-permute-start.27 = (f32[240,2560]{1,0:T(8,128)}, f32[240,2560]{1,0:T(8,128)}, u32[]{:S(2)}, u32[]{:S(2)}) collective-permute-start(f32[240,2560]{1,0:T(8,128)} %get-tuple-element.157), channel_id=1, source_target_pairs={{0,2},{1,3},{2,0},{3,1},{4,6},{5,7},{6,4},{7,5},{8,10},{9,11},{10,... | collective-permute-start | bytes 7372808 | tf_op jit(solution)/shard_map/ppermute | solution.py:400
  551.7 70.2 %collective-permute-start.28 = (f32[240,2560]{1,0:T(8,128)}, f32[240,2560]{1,0:T(8,128)}, u32[]{:S(2)}, u32[]{:S(2)}) collective-permute-start(f32[240,2560]{1,0:T(8,128)} %get-tuple-element.158), channel_id=1, source_target_pairs={{0,4},{1,5},{2,6},{3,7},{4,0},{5,1},{6,2},{7,3},{8,12},{9,13},{10,... | collective-permute-start | bytes 7372808 | tf_op jit(solution)/shard_map/ppermute | solution.py:401
  613.7 85.8 %collective-permute-start.41 = (f32[120,2560]{1,0:T(8,128)}, f32[120,2560]{1,0:T(8,128)}, u32[]{:S(2)}, u32[]{:S(2)}) collective-permute-start(f32[120,2560]{1,0:T(8,128)} %get-tuple-element.176), channel_id=1, source_target_pairs={{0,4},{1,5},{2,6},{3,7},{4,0},{5,1},{6,2},{7,3},{8,12},{9,13},{10,... | collective-permute-start | bytes 3686408 | tf_op jit(solution)/shard_map/ppermute | solution.py:404
  622.6 75.3 %collective-permute-start.32 = (f32[240,1024]{1,0:T(8,128)}, f32[240,1024]{1,0:T(8,128)}, u32[]{:S(2)}, u32[]{:S(2)}) collective-permute-start(f32[240,1024]{1,0:T(8,128)} %get-tuple-element.166), channel_id=1, source_target_pairs={{0,4},{1,5},{2,6},{3,7},{4,0},{5,1},{6,2},{7,3},{8,12},{9,13},{10,... | collective-permute-start | bytes 2949128 | tf_op jit(solution)/shard_map/ppermute | solution.py:401
  649.1 106.5 %collective-permute-start.42 = (f32[120,2560]{1,0:T(8,128)}, f32[120,2560]{1,0:T(8,128)}, u32[]{:S(2)}, u32[]{:S(2)}) collective-permute-start(f32[120,2560]{1,0:T(8,128)} %get-tuple-element.177), channel_id=1, source_target_pairs={{0,2},{1,3},{2,0},{3,1},{4,6},{5,7},{6,4},{7,5},{8,10},{9,11},{10,... | collective-permute-start | bytes 3686408 | tf_op jit(solution)/shard_map/ppermute | solution.py:405
  650.5 106.6 %collective-permute-start.43 = (f32[120,2560]{1,0:T(8,128)}, f32[120,2560]{1,0:T(8,128)}, u32[]{:S(2)}, u32[]{:S(2)}) collective-permute-start(f32[120,2560]{1,0:T(8,128)} %get-tuple-element.178), channel_id=1, source_target_pairs={{0,4},{1,5},{2,6},{3,7},{4,0},{5,1},{6,2},{7,3},{8,12},{9,13},{10,... | collective-permute-start | bytes 3686408 | tf_op jit(solution)/shard_map/ppermute | solution.py:404
  670.1 119.4 %collective-permute-start.44 = (f32[120,2560]{1,0:T(8,128)}, f32[120,2560]{1,0:T(8,128)}, u32[]{:S(2)}, u32[]{:S(2)}) collective-permute-start(f32[120,2560]{1,0:T(8,128)} %get-tuple-element.179), channel_id=1, source_target_pairs={{0,2},{1,3},{2,0},{3,1},{4,6},{5,7},{6,4},{7,5},{8,10},{9,11},{10,... | collective-permute-start | bytes 3686408 | tf_op jit(solution)/shard_map/ppermute | solution.py:405
  697.9 100.1 %collective-permute-start.45 = (f32[120,2048]{1,0:T(8,128)}, f32[120,2048]{1,0:T(8,128)}, u32[]{:S(2)}, u32[]{:S(2)}) collective-permute-start(f32[120,2048]{1,0:T(8,128)} %get-tuple-element.180), channel_id=1, source_target_pairs={{0,4},{1,5},{2,6},{3,7},{4,0},{5,1},{6,2},{7,3},{8,12},{9,13},{10,... | collective-permute-start | bytes 2949128 | tf_op jit(solution)/shard_map/ppermute | solution.py:404
  699.5 98.6 %collective-permute-start.46 = (f32[120,2048]{1,0:T(8,128)}, f32[120,2048]{1,0:T(8,128)}, u32[]{:S(2)}, u32[]{:S(2)}) collective-permute-start(f32[120,2048]{1,0:T(8,128)} %get-tuple-element.181), channel_id=1, source_target_pairs={{0,2},{1,3},{2,0},{3,1},{4,6},{5,7},{6,4},{7,5},{8,10},{9,11},{10,... | collective-permute-start | bytes 2949128 | tf_op jit(solution)/shard_map/ppermute | solution.py:405
  (62 other events, 1502.5 us)
